TPU v7x, 32 devices: a whole 2x2x4 slice. The times are simulated.
32 devices in a mesh: groups: 2 (over y), expert: 8 (over z, core), tensor: 2 (over x).
Axes of the slice: x: 2, y: 2, z: 4, core: 2. Of those that a mesh axis runs over, the one named last changes fastest.
Arguments:
- hidden_in: bfloat16 [128, 2880], P(('groups', 'expert')), parts along dimension 0, may hold values from -6 to 6
- queries: bfloat16 [128, 32, 64], P(('groups', 'expert'), 'tensor'), parts along dimension 0, may hold values from -8 to 8
- new_keys: bfloat16 [128, 8, 64], P(('groups', 'expert'), 'tensor'), parts along dimension 0, may hold values from -4 to 4
- new_values: bfloat16 [128, 8, 64], P(('groups', 'expert'), 'tensor'), parts along dimension 0, may hold values from -4 to 4
- cache_keys: bfloat16 [128, 8, 64, 256], P(('groups', 'expert'), 'tensor'), parts along dimension 0, may hold values from -8 to 8
- cache_values: bfloat16 [128, 8, 64, 256], P(('groups', 'expert'), 'tensor'), parts along dimension 0, may hold values from -4 to 4
- cache_lengths: int32 [128], P(('groups', 'expert')), parts along dimension 0, may hold values from 2 to 256, as said below
- out_weight: bfloat16 [2048, 2880], P('tensor'), may hold values from -0.125 to 0.125
- norm_gain: float32 [2880], replicated, may hold values from 0.1 to 1.9
- expert_ids: int32 [128, 4], P(('groups', 'expert')), parts along dimension 0, may hold values from 0 to 7, all different within a row; in each aligned block of 8 rows (0 to 7, 8 to 15, ...) at most 4 rows name the same one
- route_probs: float32 [128, 4], P(('groups', 'expert')), parts along dimension 0, may hold values from 0.05 to 1
- route_order: int32 [128, 4], P(('groups', 'expert')), parts along dimension 0, may hold values from 0 to 3, each once within a row
- gate_weight: bfloat16 [8, 2880, 1440], P('expert', None, 'tensor'), may hold values from -0.109375 to 0.109375
- up_weight: bfloat16 [8, 2880, 1440], P('expert', None, 'tensor'), may hold values from -0.109375 to 0.109375
- down_weight: bfloat16 [8, 1440, 2880], P('expert', 'tensor'), may hold values from -0.15625 to 0.15625
Outputs:
- layer_out: bfloat16 [128, 2880], P(('groups', 'expert'), 'tensor'), parts along dimension 0
There are 2 independent parts, one for each index of `groups`. A program takes and returns all parts, laid end to end along the dimension named above; an argument that names none is the same for every part. Nothing has to cross between parts.
Inputs may be any that keep to these rules, and one draw needn't show every extreme that they name: `cache_lengths`: some sequence fills all 256 slots. `expert_ids`: each row names 4 different experts; among the 8 rows of one device no expert is named by more than 4 rows, a bound that some block reaches. `route_order`: each row is a permutation of 0 to 3.
All inputs are finite; a program needn't handle non-finite values.
Results may differ from a plain program's by a relative error of at most 0.007.
Values may be sent and summed in bfloat16 or wider, within the bound.
No kernel may reach another device: no remote copies, remote signals or barrier semaphores. Data moves between devices by JAX's collectives and lax.ppermute only.
A program may use at most 64 MiB of HBM per device.

v0:
```python
import functools

import jax
import jax.numpy as jnp
from jax import lax
from jax.experimental import pallas as pl
from jax.experimental.pallas import tpu as pltpu
from jax.sharding import PartitionSpec as P

EPSILON = 1e-05
GLU_SLOPE = 1.702
WINDOW_FLOPS = 50_000_000_000


def attend(queries, new_keys, new_values, cache_keys, cache_values, cache_lengths):
    sequence_count, head_count, head_dim = queries.shape
    kv_heads = new_keys.shape[1]
    group_size = head_count // kv_heads
    scaling = 1.0 / head_dim**0.5
    query_rows = queries.reshape(sequence_count, kv_heads, group_size, head_dim)
    scores = (
        jnp.einsum("sgqd,sgdc->sgqc", query_rows, cache_keys, preferred_element_type=jnp.float32)
        * scaling
    )
    own_score = (
        jnp.einsum("sgqd,sgd->sgq", query_rows, new_keys, preferred_element_type=jnp.float32)
        * scaling
    )
    positions = jnp.arange(cache_keys.shape[3], dtype=jnp.int32)
    visible = positions[None, :] < cache_lengths[:, None]
    scores = jnp.where(visible[:, None, None, :], scores, -1e30)
    highest = jnp.maximum(jnp.max(scores, axis=3), own_score)
    cache_exp = jnp.exp(scores - highest[..., None])
    own_exp = jnp.exp(own_score - highest)
    totals = jnp.sum(cache_exp, axis=3) + own_exp
    cache_prob = (cache_exp / totals[..., None]).astype(jnp.bfloat16)
    own_prob = (own_exp / totals).astype(jnp.bfloat16)
    attended = jnp.einsum(
        "sgqc,sgdc->sgqd", cache_prob, cache_values, preferred_element_type=jnp.float32
    )
    attended = (
        attended
        + own_prob.astype(jnp.float32)[..., None] * new_values.astype(jnp.float32)[:, :, None, :]
    )
    return attended.astype(jnp.bfloat16).reshape(sequence_count, head_count * head_dim)


VMEM = pl.BlockSpec(memory_space=pltpu.VMEM)
LAST_DIMS = (((1,), (1,)), ((), ()))
MIB = 1 << 20


def call(kernel, outs, args, flops, moved, limit):
    return pl.pallas_call(
        kernel,
        out_shape=[jax.ShapeDtypeStruct(shape, dtype) for shape, dtype in outs],
        in_specs=[VMEM] * len(args),
        out_specs=[VMEM] * len(outs),
        compiler_params=pltpu.CompilerParams(vmem_limit_bytes=limit),
        cost_estimate=pl.CostEstimate(flops=flops, bytes_accessed=moved, transcendentals=0),
    )(*args)


def mm(left, right, dims=(((1,), (0,)), ((), ()))):
    return lax.dot_general(left, right, dims, preferred_element_type=jnp.float32)


def iota(shape, dim):
    return lax.broadcasted_iota(jnp.int32, shape, dim)


def attend_kernel(
    pieces,
    lengths_hbm,
    queries_hbm,
    new_keys_hbm,
    new_values_hbm,
    keys_hbm,
    values_hbm,
    weight_hbm,
    mine_ref,
    sent_ref,
    lengths_ref,
    queries_ref,
    new_keys_ref,
    new_values_ref,
    keys_ref,
    values_ref,
    weight_ref,
    own_keys_ref,
    own_values_ref,
    attended_ref,
    arrived,
):
    sequences, heads, head_dim = queries_ref.shape
    kv_heads = new_keys_ref.shape[1]
    group = heads // kv_heads
    span = kv_heads * head_dim
    lanes = group * head_dim
    moves = (
        (lengths_hbm, lengths_ref),
        (queries_hbm, queries_ref),
        (new_keys_hbm, new_keys_ref),
        (new_values_hbm, new_values_ref),
        (keys_hbm, keys_ref),
        (values_hbm, values_ref),
        *((weight_hbm.at[pl.ds(*piece)], weight_ref.at[pl.ds(*piece)]) for piece in pieces),
    )
    copies = [
        pltpu.make_async_copy(source, target, arrived.at[number])
        for number, (source, target) in enumerate(moves)
    ]
    for copy in copies:
        copy.start()

    rows = sequences * heads
    scaling = 1.0 / head_dim**0.5
    for copy in copies[:4]:
        copy.wait()
    queries = queries_ref[...].reshape(rows, head_dim)
    for sequence in range(sequences):
        block = pl.ds(sequence * kv_heads, kv_heads)
        own_keys_ref[block] = new_keys_ref[sequence].astype(jnp.float32)
        own_values_ref[block] = new_values_ref[sequence].astype(jnp.float32)
    own_keys = own_keys_ref[...].astype(jnp.bfloat16)
    own_values = own_values_ref[...].astype(jnp.bfloat16)

    spread = (iota((head_dim, span), 0) == iota((head_dim, span), 1) % head_dim).astype(
        jnp.bfloat16
    )
    same_head = iota((rows, span), 1) // head_dim == iota((rows, span), 0) % heads // group
    wide = jnp.where(same_head, mm(queries, spread), 0.0).astype(jnp.bfloat16)
    pairs = (rows, sequences * kv_heads)
    own_pair = iota(pairs, 1) == iota(pairs, 0) // group
    own_score = (
        jnp.sum(jnp.where(own_pair, mm(queries, own_keys, LAST_DIMS), 0.0), axis=1, keepdims=True)
        * scaling
    )

    copies[4].wait()
    slots = keys_ref.shape[2]
    scores = []
    for sequence in range(sequences):
        block = slice(sequence * heads, (sequence + 1) * heads)
        score = mm(wide[block], keys_ref[sequence]) * scaling
        visible = iota((heads, slots), 1) < lengths_ref[sequence]
        scores.append(jnp.where(visible, score, -1e30))
    scores = jnp.concatenate(scores, axis=0)
    highest = jnp.maximum(jnp.max(scores, axis=1, keepdims=True), own_score)
    cache_exp = jnp.exp(scores - highest)
    own_exp = jnp.exp(own_score - highest)
    totals = jnp.sum(cache_exp, axis=1, keepdims=True) + own_exp
    cache_prob = (cache_exp / totals).astype(jnp.bfloat16)
    own_prob = own_exp / totals
    own_prob = jnp.where(own_pair, own_prob, 0.0).astype(jnp.bfloat16)
    own_part = mm(own_prob, mm(own_values, spread).astype(jnp.bfloat16))

    copies[5].wait()
    attended = [
        mm(
            cache_prob[sequence * heads : (sequence + 1) * heads],
            values_ref[sequence],
            LAST_DIMS,
        )
        for sequence in range(sequences)
    ]
    attended = jnp.concatenate(attended, axis=0) + own_part
    attended = jnp.where(same_head, attended, 0.0).astype(jnp.bfloat16)
    repeat = (iota((span, lanes), 0) % head_dim == iota((span, lanes), 1) % head_dim).astype(
        jnp.bfloat16
    )
    own_lanes = iota((rows, lanes), 1) // head_dim == iota((rows, lanes), 0) % group
    placed = jnp.where(own_lanes, mm(attended, repeat), 0.0).astype(jnp.bfloat16)
    sums = (kv_heads * sequences, rows)
    chosen = (iota(sums, 0) % sequences == iota(sums, 1) // heads) & (
        iota(sums, 0) // sequences == iota(sums, 1) % heads // group
    )
    by_head = mm(chosen.astype(jnp.bfloat16), placed)
    for head in range(kv_heads):
        attended_ref[:, head * lanes : (head + 1) * lanes] = by_head[
            head * sequences : (head + 1) * sequences
        ].astype(jnp.bfloat16)
    attended = attended_ref[...]

    for copy, (start, size) in zip(copies[6:], pieces):
        copy.wait()
        part = mm(attended, weight_ref[pl.ds(start, size)], LAST_DIMS)
        mine_ref[:, start : start + size] = part
        sent_ref[:, start : start + size] = part.astype(jnp.bfloat16)


def attend_and_project(
    queries, new_keys, new_values, cache_keys, cache_values, cache_lengths, out_weight
):
    sequences, heads, head_dim = queries.shape
    kv_heads, slots = cache_keys.shape[1], cache_keys.shape[3]
    depth, width = out_weight.shape
    span = kv_heads * head_dim
    caches = (sequences, span, slots)
    hbm = pl.BlockSpec(memory_space=pltpu.HBM)
    arrays = (
        cache_lengths,
        queries,
        new_keys,
        new_values,
        cache_keys.reshape(caches),
        cache_values.reshape(caches),
        out_weight.T,
    )
    first = -(-width // 512) * 256
    pieces = ((0, first), (first, width - first))
    return pl.pallas_call(
        functools.partial(attend_kernel, pieces),
        out_shape=[
            jax.ShapeDtypeStruct((sequences, width), jnp.float32),
            jax.ShapeDtypeStruct((sequences, width), jnp.bfloat16),
        ],
        in_specs=[hbm] * len(arrays),
        out_specs=[VMEM] * 2,
        scratch_shapes=[pltpu.SMEM(cache_lengths.shape, cache_lengths.dtype)]
        + [pltpu.VMEM(array.shape, array.dtype) for array in arrays[1:]]
        + [
            pltpu.VMEM((sequences * kv_heads, head_dim), jnp.float32),
            pltpu.VMEM((sequences * kv_heads, head_dim), jnp.float32),
            pltpu.VMEM((sequences, depth), jnp.bfloat16),
            pltpu.SemaphoreType.DMA((len(arrays) - 1 + len(pieces),)),
        ],
        compiler_params=pltpu.CompilerParams(vmem_limit_bytes=53 * MIB),
        cost_estimate=pl.CostEstimate(
            flops=2 * sequences * width * depth,
            bytes_accessed=2 * (width * depth + 2 * sequences * span * slots),
            transcendentals=sequences * heads * slots,
        ),
    )(*[pltpu.with_memory_space_constraint(array, pltpu.HBM) for array in arrays])


def route_weights(expert_ids, route_probs, route_order, experts):
    picked = jnp.zeros(expert_ids.shape, jnp.float32)
    for column in range(expert_ids.shape[1]):
        picked = picked + jnp.where(route_order == column, route_probs[:, column : column + 1], 0.0)
    weights = picked / jnp.sum(route_probs, axis=1, keepdims=True)
    named = expert_ids[:, :, None] == jnp.arange(experts, dtype=jnp.int32)[None, None, :]
    return jnp.sum(jnp.where(named, weights[:, :, None], 0.0), axis=1)


def exchange(values, sent, axis, ranks):
    step = 1
    while True:
        pairs = [(rank, rank ^ step) for rank in range(ranks)]
        received = lax.ppermute(sent, axis, pairs)
        step *= 2
        if step >= ranks:
            return values, received
        values = values + received.astype(jnp.float32)
        sent = values.astype(jnp.bfloat16)


def table_kernel(weights_ref, table_ref):
    experts = weights_ref.shape[1]
    weights = weights_ref[...]
    high = weights.astype(jnp.bfloat16)
    low = (weights - high.astype(jnp.float32)).astype(jnp.bfloat16)
    table_ref[...] = jnp.zeros_like(table_ref)
    table_ref[:, :experts] = high
    table_ref[:, experts : 2 * experts] = low


def norm_kernel(mine_ref, received_ref, hidden_ref, gain_ref, table_ref, residual_ref, rows_ref):
    width = hidden_ref.shape[1]
    residual = (
        hidden_ref[...].astype(jnp.float32) + mine_ref[...] + received_ref[...].astype(jnp.float32)
    )
    residual_ref[...] = residual
    mean_square = jnp.mean(residual * residual, axis=1, keepdims=True)
    normed = residual * lax.rsqrt(mean_square + EPSILON) * gain_ref[...]
    rows_ref[:, :width] = normed.astype(jnp.bfloat16)
    rows_ref[:, width:] = table_ref[...]


def pack_kernel(*refs):
    *piece_refs, packed_ref = refs
    size = piece_refs[0].shape[0]
    for number, piece_ref in enumerate(piece_refs):
        packed_ref[pl.ds(number * size, size)] = piece_ref[...]


def turn_kernel(*refs):
    for source_ref, target_ref in zip(refs[: len(refs) // 2], refs[len(refs) // 2 :]):
        for local in range(source_ref.shape[0]):
            target_ref[local] = source_ref[local].T


def turn(*weights):
    return call(
        turn_kernel,
        [(weight.shape, weight.dtype) for weight in weights],
        [weight.swapaxes(1, 2) for weight in weights],
        flops=1,
        moved=1,
        limit=6 * MIB,
    )


def expert_kernel(experts, *refs):
    *row_refs, gate_ref, up_ref, down_ref, mine_ref, other_ref = refs
    local_experts, _, width = down_ref.shape
    rows = jnp.concatenate([ref[:, :width] for ref in row_refs], axis=0)
    table = jnp.concatenate([ref[:, width:] for ref in row_refs], axis=0).astype(jnp.float32)
    column = lax.broadcasted_iota(jnp.int32, table.shape, 1)
    total = None
    for local in range(local_experts):
        expert = lax.axis_index("expert") * local_experts + local
        chosen = (column == expert) | (column == expert + experts)
        weight = jnp.sum(jnp.where(chosen, table, 0.0), axis=1, keepdims=True)
        gate = mm(rows, gate_ref[local])
        up = mm(rows, up_ref[local])
        active = (gate * jax.nn.sigmoid(GLU_SLOPE * gate) * (up + 1.0)).astype(jnp.bfloat16)
        part = mm(active, down_ref[local])
        part = part * weight
        total = part if total is None else total + part
    half = mine_ref.shape[0]
    mine_ref[...] = total[:half]
    other_ref[...] = total[half:].astype(jnp.bfloat16)


def split_kernel(mine_ref, received_ref, kept_ref, *sent_refs):
    size = kept_ref.shape[0]
    kept_ref[...] = mine_ref[:size] + received_ref[:size].astype(jnp.float32)
    for number, sent_ref in enumerate(sent_refs, 1):
        block = pl.ds(number * size, size)
        total = mine_ref[block] + received_ref[block].astype(jnp.float32)
        sent_ref[...] = total.astype(jnp.bfloat16)


def return_kernel(received, residual_ref, *refs):
    kept_ref, *received_refs = refs[: 1 + received]
    base_ref, *sent_refs = refs[1 + received :]
    total = kept_ref[...]
    for received_ref in received_refs:
        total = total + received_ref[...].astype(jnp.float32)
    width = base_ref.shape[1]
    rank = lax.axis_index("tensor")

    def slab_of(values, owner):
        slab = values[:, :width]
        for number in range(1, values.shape[1] // width):
            piece = values[:, number * width : (number + 1) * width]
            slab = jnp.where(owner == number, piece, slab)
        return slab

    base_ref[...] = slab_of(total + residual_ref[...], rank)
    for step, sent_ref in enumerate(sent_refs, 1):
        sent_ref[...] = slab_of(total, rank ^ step).astype(jnp.bfloat16)


def per_device(
    hidden_in,
    queries,
    new_keys,
    new_values,
    cache_keys,
    cache_values,
    cache_lengths,
    out_weight,
    norm_gain,
    expert_ids,
    route_probs,
    route_order,
    gate_weight,
    up_weight,
    down_weight,
):
    sequences, width = hidden_in.shape
    expert_ranks = lax.axis_size("expert")
    tensor_ranks = lax.axis_size("tensor")
    local_experts, hidden_units = down_weight.shape[:2]
    experts = local_experts * expert_ranks
    inner = 2
    outer = expert_ranks // inner
    row_width = -(-(width + 2 * experts) // 128) * 128

    def to_outer(values, step):
        pairs = [(rank, rank ^ (step * inner)) for rank in range(expert_ranks)]
        return lax.ppermute(values, "expert", pairs)

    def to_inner(values):
        return lax.ppermute(values, "expert", [(rank, rank ^ 1) for rank in range(expert_ranks)])

    operands = (queries, new_keys, new_values, cache_keys, cache_values, cache_lengths)
    if queries.shape[1] % 16 == 0:
        mine, sent = attend_and_project(*operands, out_weight)
    else:
        mine = jnp.dot(attend(*operands), out_weight, preferred_element_type=jnp.float32)
        sent = mine.astype(jnp.bfloat16)
    mine, received = exchange(mine, sent, "tensor", tensor_ranks)

    weights = route_weights(expert_ids, route_probs, route_order, experts)
    (table,) = call(
        table_kernel,
        [((sequences, row_width - width), jnp.bfloat16)],
        (weights,),
        flops=WINDOW_FLOPS,
        moved=sequences * row_width,
        limit=MIB,
    )

    block = (sequences, width)
    residual, rows = call(
        norm_kernel,
        [(block, jnp.float32), ((sequences, row_width), jnp.bfloat16)],
        (mine, received, hidden_in, norm_gain.reshape(1, width), table),
        flops=16 * sequences * width,
        moved=sequences * width * 16,
        limit=2 * MIB,
    )

    near = [rows]
    for step in range(1, outer):
        near.append(to_outer(rows, step))
    gate_weight, up_weight = turn(gate_weight, up_weight)
    (near,) = call(
        pack_kernel,
        [((outer * sequences, row_width), jnp.bfloat16)],
        near,
        flops=sequences,
        moved=4 * outer * sequences * row_width,
        limit=2 * MIB,
    )
    far = to_inner(near)
    half = (outer * sequences, width)
    mine, other = call(
        functools.partial(expert_kernel, experts),
        [(half, jnp.float32), (half, jnp.bfloat16)],
        (near, far, gate_weight, up_weight, down_weight),
        flops=12 * half[0] * width * hidden_units * local_experts,
        moved=6 * width * hidden_units * local_experts,
        limit=16 * MIB,
    )
    received = to_inner(other)
    kept, *sent = call(
        split_kernel,
        [(block, jnp.float32)] + [(block, jnp.bfloat16)] * (outer - 1),
        (mine, received),
        flops=half[0] * width,
        moved=half[0] * width * 8,
        limit=4 * MIB,
    )
    returned = []
    for step, piece in enumerate(sent, 1):
        returned.append(to_outer(piece, step))
    slab = (sequences, width // tensor_ranks)
    total, *sent = call(
        functools.partial(return_kernel, len(returned)),
        [(slab, jnp.float32)] + [(slab, jnp.bfloat16)] * (tensor_ranks - 1),
        (residual, kept, *returned),
        flops=half[0] * width,
        moved=half[0] * width * 2,
        limit=2 * MIB,
    )
    for step, piece in enumerate(sent, 1):
        pairs = [(rank, rank ^ step) for rank in range(tensor_ranks)]
        total = total + lax.ppermute(piece, "tensor", pairs).astype(jnp.float32)
    return total.astype(jnp.bfloat16)


def solution(mesh):
    in_specs = (
        P(("groups", "expert"), None),
        P(("groups", "expert"), "tensor", None),
        P(("groups", "expert"), "tensor", None),
        P(("groups", "expert"), "tensor", None),
        P(("groups", "expert"), "tensor", None, None),
        P(("groups", "expert"), "tensor", None, None),
        P(("groups", "expert")),
        P("tensor", None),
        P(),
        P(("groups", "expert"), None),
        P(("groups", "expert"), None),
        P(("groups", "expert"), None),
        P("expert", None, "tensor"),
        P("expert", None, "tensor"),
        P("expert", "tensor", None),
    )
    out_specs = P(("groups", "expert"), "tensor")

    return jax.shard_map(
        per_device, mesh=mesh, in_specs=in_specs, out_specs=out_specs, check_vma=False
    )
```

profile of v0, /device:TPU:0, one launch (start us, length us, event | category | flops | bytes accessed | tf_op | source)
XLA Modules:
  0.0 38.6 jit_solution(4293832791394001352)
XLA Ops:
  0.0 0.0 copy-start.3
  0.0 0.0 copy-start.4
  0.0 0.0 copy-start.5
  0.0 0.0 slice-start
  0.0 4.8 %shard_map.145 = (f32[8,2880]{1,0:T(8,128)S(1)}, bf16[8,2880]{1,0:T(8,128)(2,1)S(1)}) custom-call(s32[8]{0:T(128)} %lengths_hbm.1, bf16[8,16,64]{2,1,0:T(8,128)(2,1)} %queries_hbm.1, bf16[8,4,64]{2,1,0:T(4,128)(2,1)} %new_keys_hbm.1, bf16[8,4,64]{2,1,0:T(4,128)(2,1)} %new_values_hbm.1, bf16[8,256,256]{2,1,0:T(8,128)(2,1)} %bitcast.20, ...), custom_call_target="tpu_custom_call" | custom-call | flops 47185920 | bytes 7995392 | tf_op jit(solution)/shard_map/pallas_call | solution.py:212
  4.8 3.0 %collective-permute-start = (bf16[8,2880]{1,0:T(8,128)(2,1)S(1)}, bf16[8,2880]{1,0:T(8,128)(2,1)S(1)}, u32[]{:S(2)}, u32[]{:S(2)}) collective-permute-start(bf16[8,2880]{1,0:T(8,128)(2,1)S(1)} %get-tuple-element.20), channel_id=1, source_target_pairs={{0,1},{1,0},{2,3},{3,2},{4,5},{5,4},{6,7},{7,6},{8,9},{9,8},{10,11... | collective-permute-start | bytes 138248 | tf_op jit(solution)/shard_map/ppermute | solution.py:250
  7.9 0.0 copy-done.3
  7.9 0.0 copy-done.4
  7.9 0.0 copy-done.5
  7.9 0.1 select_reduce_fusion.weights_ref
  8.0 0.0 copy-start.2
  8.0 0.0 copy-start.1
  8.0 0.0 slice-start.1
  8.1 0.0 copy-start
  8.1 0.1 shard_map.146.table_ref
  8.1 0.6 %copy-done.2 = f32[2880]{0:T(1024)S(1)} copy-done((f32[2880]{0:T(1024)S(1)}, f32[2880]{0:T(1024)}, u32[]{:S(2)}) %copy-start.2) | copy-done | bytes 11544
  8.7 1.2 %collective-permute-done.received_ref = bf16[8,2880]{1,0:T(8,128)(2,1)S(1)} collective-permute-done((bf16[8,2880]{1,0:T(8,128)(2,1)S(1)}, bf16[8,2880]{1,0:T(8,128)(2,1)S(1)}, u32[]{:S(2)}, u32[]{:S(2)}) %collective-permute-start) | collective-permute-done | bytes 46112 | tf_op jit(solution)/shard_map/ppermute | solution.py:250
  9.9 0.0 copy-done.1
  9.9 0.1 shard_map.147
  10.1 0.0 slice-start.2
  10.1 4.2 %collective-permute-start.3 = (bf16[8,2944]{1,0:T(8,128)(2,1)S(1)}, bf16[8,2944]{1,0:T(8,128)(2,1)S(1)}, u32[]{:S(2)}, u32[]{:S(2)}) collective-permute-start(bf16[8,2944]{1,0:T(8,128)(2,1)S(1)} %get-tuple-element.22.refs_0_), channel_id=1, source_target_pairs={{0,12},{2,14},{4,8},{6,10},{8,4},{10,6},{12,0},{14,2},{1,13},{3,15... | collective-permute-start | bytes 141320 | tf_op jit(solution)/shard_map/ppermute | solution.py:384
  14.3 0.0 collective-permute-start.2
  14.3 0.6 %collective-permute-start.1 = (bf16[8,2944]{1,0:T(8,128)(2,1)S(1)}, bf16[8,2944]{1,0:T(8,128)(2,1)S(1)}, u32[]{:S(2)}, u32[]{:S(2)}) collective-permute-start(bf16[8,2944]{1,0:T(8,128)(2,1)S(1)} %get-tuple-element.22.refs_0_), channel_id=1, source_target_pairs={{0,4},{2,6},{4,0},{6,2},{8,12},{10,14},{12,8},{14,10},{1,5},{3,7},... | collective-permute-start | bytes 141320 | tf_op jit(solution)/shard_map/ppermute | solution.py:384
  14.9 1.4 %collective-permute-done.3.refs_3_ = bf16[8,2944]{1,0:T(8,128)(2,1)S(1)} collective-permute-done((bf16[8,2944]{1,0:T(8,128)(2,1)S(1)}, bf16[8,2944]{1,0:T(8,128)(2,1)S(1)}, u32[]{:S(2)}, u32[]{:S(2)}) %collective-permute-start.3) | collective-permute-done | bytes 47136 | tf_op jit(solution)/shard_map/ppermute | solution.py:384
  16.3 2.9 %collective-permute-done.2.refs_2_ = bf16[8,2944]{1,0:T(8,128)(2,1)S(1)} collective-permute-done((bf16[8,2944]{1,0:T(8,128)(2,1)S(1)}, bf16[8,2944]{1,0:T(8,128)(2,1)S(1)}, u32[]{:S(2)}, u32[]{:S(2)}) %collective-permute-start.2) | collective-permute-done | bytes 47136 | tf_op jit(solution)/shard_map/ppermute | solution.py:384
  19.2 0.0 collective-permute-done.1.refs_1_
  19.3 0.1 collective-permute-start.4
  19.3 0.0 slice-done
  19.4 0.0 slice-done.1
  19.4 0.0 copy-done
  19.4 0.0 slice-start.3
  19.4 2.4 %shard_map.149 = (bf16[1,2880,720]{2,1,0:T(8,128)(2,1)S(1)}, bf16[1,2880,720]{2,1,0:T(8,128)(2,1)S(1)}) custom-call(bf16[1,720,2880]{2,1,0:T(8,128)(2,1)S(1)} %bitcast.15, bf16[1,720,2880]{2,1,0:T(8,128)(2,1)S(1)} %bitcast.16), custom_call_target="tpu_custom_call" | custom-call | flops 1 | bytes 1 | tf_op jit(solution)/shard_map/pallas_call | solution.py:54
  21.8 0.0 collective-permute-done.4.refs_1_
  21.8 0.0 slice-done.2
  21.8 0.0 slice-done.3
  21.9 2.3 %shard_map.150 = (f32[32,2880]{1,0:T(8,128)S(1)}, bf16[32,2880]{1,0:T(8,128)(2,1)S(1)}) custom-call(bf16[32,2944]{1,0:T(8,128)(2,1)S(1)} %shard_map.148.refs_0_, bf16[32,2944]{1,0:T(8,128)(2,1)S(1)} %collective-permute-done.4.refs_1_, bf16[1,2880,720]{2,1,0:T(8,128)(2,1)S(1)} %get-tuple-element.23.refs_2_, ...), custom_call_target="tpu_custom_call" | custom-call | flops 796262400 | bytes 12441600 | tf_op jit(solution)/shard_map/pallas_call | solution.py:54
  24.2 0.5 %collective-permute-start.5 = (bf16[32,2880]{1,0:T(8,128)(2,1)S(1)}, bf16[32,2880]{1,0:T(8,128)(2,1)S(1)}, u32[]{:S(2)}, u32[]{:S(2)}) collective-permute-start(bf16[32,2880]{1,0:T(8,128)(2,1)S(1)} %get-tuple-element.26), channel_id=1, source_target_pairs={{0,2},{2,0},{4,6},{6,4},{8,10},{10,8},{12,14},{14,12},{1,3},{3,1},... | collective-permute-start | bytes 552968 | tf_op jit(solution)/shard_map/ppermute | solution.py:387
  24.7 1.1 %collective-permute-done.5.received_ref = bf16[32,2880]{1,0:T(8,128)(2,1)S(1)} collective-permute-done((bf16[32,2880]{1,0:T(8,128)(2,1)S(1)}, bf16[32,2880]{1,0:T(8,128)(2,1)S(1)}, u32[]{:S(2)}, u32[]{:S(2)}) %collective-permute-start.5) | collective-permute-done | bytes 184352 | tf_op jit(solution)/shard_map/ppermute | solution.py:387
  25.8 0.2 collective-permute-start.6
  26.0 2.0 %collective-permute-start.7 = (bf16[8,2880]{1,0:T(8,128)(2,1)S(1)}, bf16[8,2880]{1,0:T(8,128)(2,1)S(1)}, u32[]{:S(2)}, u32[]{:S(2)}) collective-permute-start(bf16[8,2880]{1,0:T(8,128)(2,1)S(1)} %get-tuple-element.29), channel_id=1, source_target_pairs={{0,8},{2,10},{4,12},{6,14},{8,0},{10,2},{12,4},{14,6},{1,9},{3,11}... | collective-permute-start | bytes 138248 | tf_op jit(solution)/shard_map/ppermute | solution.py:384
  28.0 2.3 %collective-permute-start.8 = (bf16[8,2880]{1,0:T(8,128)(2,1)S(1)}, bf16[8,2880]{1,0:T(8,128)(2,1)S(1)}, u32[]{:S(2)}, u32[]{:S(2)}) collective-permute-start(bf16[8,2880]{1,0:T(8,128)(2,1)S(1)} %get-tuple-element.30), channel_id=1, source_target_pairs={{0,12},{2,14},{4,8},{6,10},{8,4},{10,6},{12,0},{14,2},{1,13},{3,15... | collective-permute-start | bytes 138248 | tf_op jit(solution)/shard_map/ppermute | solution.py:384
  30.3 0.7 %collective-permute-done.6.refs_1_ = bf16[8,2880]{1,0:T(8,128)(2,1)S(1)} collective-permute-done((bf16[8,2880]{1,0:T(8,128)(2,1)S(1)}, bf16[8,2880]{1,0:T(8,128)(2,1)S(1)}, u32[]{:S(2)}, u32[]{:S(2)}) %collective-permute-start.6) | collective-permute-done | bytes 46112 | tf_op jit(solution)/shard_map/ppermute | solution.py:384
  31.0 0.0 collective-permute-done.7.refs_2_
  31.0 2.9 %collective-permute-done.8.refs_3_ = bf16[8,2880]{1,0:T(8,128)(2,1)S(1)} collective-permute-done((bf16[8,2880]{1,0:T(8,128)(2,1)S(1)}, bf16[8,2880]{1,0:T(8,128)(2,1)S(1)}, u32[]{:S(2)}, u32[]{:S(2)}) %collective-permute-start.8) | collective-permute-done | bytes 46112 | tf_op jit(solution)/shard_map/ppermute | solution.py:384
  33.9 0.2 shard_map.152
  34.0 1.6 %collective-permute-start.9 = (bf16[8,1440]{1,0:T(8,128)(2,1)S(1)}, bf16[8,1440]{1,0:T(8,128)(2,1)S(1)}, u32[]{:S(2)}, u32[]{:S(2)}) collective-permute-start(bf16[8,1440]{1,0:T(8,128)(2,1)S(1)} %get-tuple-element.32), channel_id=1, source_target_pairs={{0,1},{1,0},{2,3},{3,2},{4,5},{5,4},{6,7},{7,6},{8,9},{9,8},{10,11... | collective-permute-start | bytes 69128 | tf_op jit(solution)/shard_map/ppermute | solution.py:462
  35.6 2.3 %collective-permute-done.9 = bf16[8,1440]{1,0:T(8,128)(2,1)S(1)} collective-permute-done((bf16[8,1440]{1,0:T(8,128)(2,1)S(1)}, bf16[8,1440]{1,0:T(8,128)(2,1)S(1)}, u32[]{:S(2)}, u32[]{:S(2)}) %collective-permute-start.9) | collective-permute-done | bytes 23072 | tf_op jit(solution)/shard_map/ppermute | solution.py:462
  37.9 0.6 %add_convert_fusion = bf16[8,1440]{1,0:T(8,128)(2,1)} fusion(f32[8,1440]{1,0:T(8,128)S(1)} %get-tuple-element.31, bf16[8,1440]{1,0:T(8,128)(2,1)S(1)} %collective-permute-done.9), kind=kLoop, calls=%fused_computation | loop fusion | flops 34560 | bytes 92160 | tf_op jit(solution)/shard_map/convert_element_type | solution.py:463
  (8 shorter events, 0.1 us)
Async XLA Ops:
  0.0 7.9 %copy-start.3 = (f32[8,4]{0,1:T(4,128)S(1)}, f32[8,4]{0,1:T(4,128)}, u32[]{:S(2)}) copy-start(f32[8,4]{0,1:T(4,128)} %param.25) | copy-start | bytes 388
  0.0 7.9 %copy-start.4 = (s32[8,4]{0,1:T(4,128)S(1)}, s32[8,4]{0,1:T(4,128)}, u32[]{:S(2)}) copy-start(s32[8,4]{0,1:T(4,128)} %param.26) | copy-start | bytes 388
  0.0 7.9 %copy-start.5 = (s32[8,4]{0,1:T(4,128)S(1)}, s32[8,4]{0,1:T(4,128)}, u32[]{:S(2)}) copy-start(s32[8,4]{0,1:T(4,128)} %param.24) | copy-start | bytes 388
  0.0 19.3 %slice-start = ((s8[4239360]{0:T(1024)(128)(4,1)}), s8[45056]{0:T(1024)(128)(4,1)S(1)}, s32[]{:S(2)}) async-start(s8[4239360]{0:T(1024)(128)(4,1)} %bitcast.13), calls=%async_computation | async-start | bytes 90112
  4.8 5.1 %collective-permute-start = (bf16[8,2880]{1,0:T(8,128)(2,1)S(1)}, bf16[8,2880]{1,0:T(8,128)(2,1)S(1)}, u32[]{:S(2)}, u32[]{:S(2)}) collective-permute-start(bf16[8,2880]{1,0:T(8,128)(2,1)S(1)} %get-tuple-element.20), channel_id=1, source_target_pairs={{0,1},{1,0},{2,3},{3,2},{4,5},{5,4},{6,7},{7,6},{8,9},{9,8},{10,11... | collective-permute-start | bytes 138248 | tf_op jit(solution)/shard_map/ppermute | solution.py:250
  8.0 0.7 %copy-start.2 = (f32[2880]{0:T(1024)S(1)}, f32[2880]{0:T(1024)}, u32[]{:S(2)}) copy-start(f32[2880]{0:T(1024)} %param.23) | copy-start | bytes 34564
  8.0 1.9 %copy-start.1 = (bf16[8,2880]{1,0:T(8,128)(2,1)S(1)}, bf16[8,2880]{1,0:T(8,128)(2,1)}, u32[]{:S(2)}) copy-start(bf16[8,2880]{1,0:T(8,128)(2,1)} %hidden_ref.1) | copy-start | bytes 138244
  8.0 11.3 %slice-start.1 = ((s8[4239360]{0:T(1024)(128)(4,1)}), s8[4194304]{0:T(1024)(128)(4,1)S(1)}, s32[]{:S(2)}) async-start(s8[4239360]{0:T(1024)(128)(4,1)} %bitcast.13), calls=%async_computation.1 | async-start | bytes 8388608
  8.1 11.3 %copy-start = (bf16[1,2880,720]{1,2,0:T(8,128)(2,1)S(1)}, bf16[1,2880,720]{1,2,0:T(8,128)(2,1)}, u32[]{:S(2)}) copy-start(bf16[1,2880,720]{1,2,0:T(8,128)(2,1)} %param.28) | copy-start | bytes 12441604
  10.1 11.8 %slice-start.2 = ((s8[4239360]{0:T(1024)(128)(4,1)}), s8[4194304]{0:T(1024)(128)(4,1)S(1)}, s32[]{:S(2)}) async-start(s8[4239360]{0:T(1024)(128)(4,1)} %bitcast.17), calls=%async_computation.2 | async-start | bytes 8388608
  10.1 6.2 %collective-permute-start.3 = (bf16[8,2944]{1,0:T(8,128)(2,1)S(1)}, bf16[8,2944]{1,0:T(8,128)(2,1)S(1)}, u32[]{:S(2)}, u32[]{:S(2)}) collective-permute-start(bf16[8,2944]{1,0:T(8,128)(2,1)S(1)} %get-tuple-element.22.refs_0_), channel_id=1, source_target_pairs={{0,12},{2,14},{4,8},{6,10},{8,4},{10,6},{12,0},{14,2},{1,13},{3,15... | collective-permute-start | bytes 141320 | tf_op jit(solution)/shard_map/ppermute | solution.py:384
  14.3 5.0 %collective-permute-start.2 = (bf16[8,2944]{1,0:T(8,128)(2,1)S(1)}, bf16[8,2944]{1,0:T(8,128)(2,1)S(1)}, u32[]{:S(2)}, u32[]{:S(2)}) collective-permute-start(bf16[8,2944]{1,0:T(8,128)(2,1)S(1)} %get-tuple-element.22.refs_0_), channel_id=1, source_target_pairs={{0,8},{2,10},{4,12},{6,14},{8,0},{10,2},{12,4},{14,6},{1,9},{3,11}... | collective-permute-start | bytes 141320 | tf_op jit(solution)/shard_map/ppermute | solution.py:384
  14.3 5.0 %collective-permute-start.1 = (bf16[8,2944]{1,0:T(8,128)(2,1)S(1)}, bf16[8,2944]{1,0:T(8,128)(2,1)S(1)}, u32[]{:S(2)}, u32[]{:S(2)}) collective-permute-start(bf16[8,2944]{1,0:T(8,128)(2,1)S(1)} %get-tuple-element.22.refs_0_), channel_id=1, source_target_pairs={{0,4},{2,6},{4,0},{6,2},{8,12},{10,14},{12,8},{14,10},{1,5},{3,7},... | collective-permute-start | bytes 141320 | tf_op jit(solution)/shard_map/ppermute | solution.py:384
  19.3 2.5 %collective-permute-start.4 = (bf16[32,2944]{1,0:T(8,128)(2,1)S(1)}, bf16[32,2944]{1,0:T(8,128)(2,1)S(1)}, u32[]{:S(2)}, u32[]{:S(2)}) collective-permute-start(bf16[32,2944]{1,0:T(8,128)(2,1)S(1)} %shard_map.148.refs_0_), channel_id=1, source_target_pairs={{0,2},{2,0},{4,6},{6,4},{8,10},{10,8},{12,14},{14,12},{1,3},{3,1},... | collective-permute-start | bytes 565256 | tf_op jit(solution)/shard_map/ppermute | solution.py:387
  19.4 2.5 %slice-start.3 = ((s8[4239360]{0:T(1024)(128)(4,1)}), s8[45056]{0:T(1024)(128)(4,1)S(1)}, s32[]{:S(2)}) async-start(s8[4239360]{0:T(1024)(128)(4,1)} %bitcast.17), calls=%async_computation.3 | async-start | bytes 90112
  24.2 1.6 %collective-permute-start.5 = (bf16[32,2880]{1,0:T(8,128)(2,1)S(1)}, bf16[32,2880]{1,0:T(8,128)(2,1)S(1)}, u32[]{:S(2)}, u32[]{:S(2)}) collective-permute-start(bf16[32,2880]{1,0:T(8,128)(2,1)S(1)} %get-tuple-element.26), channel_id=1, source_target_pairs={{0,2},{2,0},{4,6},{6,4},{8,10},{10,8},{12,14},{14,12},{1,3},{3,1},... | collective-permute-start | bytes 552968 | tf_op jit(solution)/shard_map/ppermute | solution.py:387
  25.8 5.1 %collective-permute-start.6 = (bf16[8,2880]{1,0:T(8,128)(2,1)S(1)}, bf16[8,2880]{1,0:T(8,128)(2,1)S(1)}, u32[]{:S(2)}, u32[]{:S(2)}) collective-permute-start(bf16[8,2880]{1,0:T(8,128)(2,1)S(1)} %get-tuple-element.28), channel_id=1, source_target_pairs={{0,4},{2,6},{4,0},{6,2},{8,12},{10,14},{12,8},{14,10},{1,5},{3,7},... | collective-permute-start | bytes 138248 | tf_op jit(solution)/shard_map/ppermute | solution.py:384
  26.0 5.0 %collective-permute-start.7 = (bf16[8,2880]{1,0:T(8,128)(2,1)S(1)}, bf16[8,2880]{1,0:T(8,128)(2,1)S(1)}, u32[]{:S(2)}, u32[]{:S(2)}) collective-permute-start(bf16[8,2880]{1,0:T(8,128)(2,1)S(1)} %get-tuple-element.29), channel_id=1, source_target_pairs={{0,8},{2,10},{4,12},{6,14},{8,0},{10,2},{12,4},{14,6},{1,9},{3,11}... | collective-permute-start | bytes 138248 | tf_op jit(solution)/shard_map/ppermute | solution.py:384
  28.0 5.9 %collective-permute-start.8 = (bf16[8,2880]{1,0:T(8,128)(2,1)S(1)}, bf16[8,2880]{1,0:T(8,128)(2,1)S(1)}, u32[]{:S(2)}, u32[]{:S(2)}) collective-permute-start(bf16[8,2880]{1,0:T(8,128)(2,1)S(1)} %get-tuple-element.30), channel_id=1, source_target_pairs={{0,12},{2,14},{4,8},{6,10},{8,4},{10,6},{12,0},{14,2},{1,13},{3,15... | collective-permute-start | bytes 138248 | tf_op jit(solution)/shard_map/ppermute | solution.py:384
  34.0 3.9 %collective-permute-start.9 = (bf16[8,1440]{1,0:T(8,128)(2,1)S(1)}, bf16[8,1440]{1,0:T(8,128)(2,1)S(1)}, u32[]{:S(2)}, u32[]{:S(2)}) collective-permute-start(bf16[8,1440]{1,0:T(8,128)(2,1)S(1)} %get-tuple-element.32), channel_id=1, source_target_pairs={{0,1},{1,0},{2,3},{3,2},{4,5},{5,4},{6,7},{7,6},{8,9},{9,8},{10,11... | collective-permute-start | bytes 69128 | tf_op jit(solution)/shard_map/ppermute | solution.py:462
where the time goes:
time: 38.8 us; the launch traced here: 38.6 us
  starting transfers between devices  14.5 us (37%)
  waiting for transfers between devices  12.5 us (32%)
  Pallas kernels  9.99 us (26%)
  other arithmetic  0.72 us (2%)
  local copies, waits for them, and re-layouts  0.65 us (2%)
    ppermute x6, starting transfers between devices, to_outer(): return lax.ppermute(values, 'expert', pairs)  9.29 us
    ppermute x6, waiting for transfers between devices, to_outer(): return lax.ppermute(values, 'expert', pairs)  7.9 us
    pallas_call x7, Pallas kernels, call(): pl.pallas_call(kernel, out_shape=[jax.ShapeDtypeStruct(shape, dtype) for...  5.17 us
    pallas_call x1, Pallas kernels, attend_and_project(): pl.pallas_call(functools.partial(attend_kernel, pieces), out_shape=[jax.S...  4.82 us
    ppermute x1, starting transfers between devices, exchange(): received = lax.ppermute(sent, axis, pairs)  3.05 us
    ppermute x1, waiting for transfers between devices, per_device(): total = total + lax.ppermute(piece, 'tensor', pairs).astype(jnp.float32)  2.34 us
    ppermute x1, starting transfers between devices, per_device(): total = total + lax.ppermute(piece, 'tensor', pairs).astype(jnp.float32)  1.55 us
    ppermute x1, waiting for transfers between devices, exchange(): received = lax.ppermute(sent, axis, pairs)  1.19 us
  transfers between devices with their start and end apart: 10, of which 7 were waited for; matrix products, arithmetic and copies ran while one was open for 0% of the time, Pallas kernels for 6%

commit v1 on v0

--- a/solution.py
+++ b/solution.py
@@ -284,16 +284,20 @@
         packed_ref[pl.ds(number * size, size)] = piece_ref[...]
 
 
-def turn_kernel(*refs):
-    for source_ref, target_ref in zip(refs[: len(refs) // 2], refs[len(refs) // 2 :]):
+def turn_kernel(pieces, *refs):
+    for (start, size), source_ref, target_ref in zip(
+        pieces, refs[: len(pieces)], refs[len(pieces) :]
+    ):
         for local in range(source_ref.shape[0]):
-            target_ref[local] = source_ref[local].T
-
-
-def turn(*weights):
+            target_ref[local] = source_ref[local, pl.ds(start, size)].T
+
+
+def turn(*sources):
+    weights = [weight for weight, _, _ in sources]
+    pieces = [(start, size) for _, start, size in sources]
     return call(
-        turn_kernel,
-        [(weight.shape, weight.dtype) for weight in weights],
+        functools.partial(turn_kernel, pieces),
+        [(weight.shape[:2] + (size,), weight.dtype) for weight, _, size in sources],
         [weight.swapaxes(1, 2) for weight in weights],
         flops=1,
         moved=1,
@@ -302,7 +306,7 @@
 
 
 def expert_kernel(experts, *refs):
-    *row_refs, gate_ref, up_ref, down_ref, mine_ref, other_ref = refs
+    *row_refs, gate_ref, first_ref, second_ref, down_ref, mine_ref, other_ref = refs
     local_experts, _, width = down_ref.shape
     rows = jnp.concatenate([ref[:, :width] for ref in row_refs], axis=0)
     table = jnp.concatenate([ref[:, width:] for ref in row_refs], axis=0).astype(jnp.float32)
@@ -312,10 +316,16 @@
         expert = lax.axis_index("expert") * local_experts + local
         chosen = (column == expert) | (column == expert + experts)
         weight = jnp.sum(jnp.where(chosen, table, 0.0), axis=1, keepdims=True)
-        gate = mm(rows, gate_ref[local])
-        up = mm(rows, up_ref[local])
-        active = (gate * jax.nn.sigmoid(GLU_SLOPE * gate) * (up + 1.0)).astype(jnp.bfloat16)
-        part = mm(active, down_ref[local])
+        part = None
+        start = 0
+        for up_ref in (first_ref, second_ref):
+            piece = pl.ds(start, up_ref.shape[2])
+            gate = mm(rows, gate_ref[local, :, piece])
+            up = mm(rows, up_ref[local])
+            active = (gate * jax.nn.sigmoid(GLU_SLOPE * gate) * (up + 1.0)).astype(jnp.bfloat16)
+            term = mm(active, down_ref[local, piece])
+            part = term if part is None else part + term
+            start += up_ref.shape[2]
         part = part * weight
         total = part if total is None else total + part
     half = mine_ref.shape[0]
@@ -377,6 +387,7 @@
     experts = local_experts * expert_ranks
     inner = 2
     outer = expert_ranks // inner
+    cut = 3 * hidden_units // 4 // 128 * 128
     row_width = -(-(width + 2 * experts) // 128) * 128
 
     def to_outer(values, step):
@@ -417,7 +428,7 @@
     near = [rows]
     for step in range(1, outer):
         near.append(to_outer(rows, step))
-    gate_weight, up_weight = turn(gate_weight, up_weight)
+    gate_turned, up_first = turn((gate_weight, 0, hidden_units), (up_weight, 0, cut))
     (near,) = call(
         pack_kernel,
         [((outer * sequences, row_width), jnp.bfloat16)],
@@ -427,11 +438,12 @@
         limit=2 * MIB,
     )
     far = to_inner(near)
+    (up_second,) = turn((up_weight, cut, hidden_units - cut))
     half = (outer * sequences, width)
     mine, other = call(
         functools.partial(expert_kernel, experts),
         [(half, jnp.float32), (half, jnp.bfloat16)],
-        (near, far, gate_weight, up_weight, down_weight),
+        (near, far, gate_turned, up_first, up_second, down_weight),
         flops=12 * half[0] * width * hidden_units * local_experts,
         moved=6 * width * hidden_units * local_experts,
         limit=16 * MIB,

time: 38.8 us -> 38.9 us (level)
    unnamed x20 -> x22, local copies, waits for them, and re-layouts: 0.64 us -> 0.8 us
    pallas_call x7 -> x8, Pallas kernels: 5.17 us -> 5.33 us  [call(): pl.pallas_call(kernel, out_shape=[jax.ShapeDtypeStruct(shape, dtype) for...]
  transfers between devices with their start and end apart: 10 -> 10, of which waited for: 7 -> 8; matrix products, arithmetic and copies ran while one was open for 0% -> 0% of each run, Pallas kernels for 6% -> 7%
where the time goes in v1:
time: 38.9 us; the launch traced here: 38.7 us
  starting transfers between devices  14.5 us (37%)
  waiting for transfers between devices  12.3 us (32%)
  Pallas kernels  10.1 us (26%)
  local copies, waits for them, and re-layouts  0.81 us (2%)
  other arithmetic  0.72 us (2%)
    ppermute x6, starting transfers between devices, to_outer(): return lax.ppermute(values, 'expert', pairs)  9.29 us
    ppermute x6, waiting for transfers between devices, to_outer(): return lax.ppermute(values, 'expert', pairs)  7.91 us
    pallas_call x8, Pallas kernels, call(): pl.pallas_call(kernel, out_shape=[jax.ShapeDtypeStruct(shape, dtype) for...  5.33 us
    pallas_call x1, Pallas kernels, attend_and_project(): pl.pallas_call(functools.partial(attend_kernel, pieces), out_shape=[jax.S...  4.82 us
    ppermute x1, starting transfers between devices, exchange(): received = lax.ppermute(sent, axis, pairs)  3.05 us
    ppermute x1, waiting for transfers between devices, per_device(): total = total + lax.ppermute(piece, 'tensor', pairs).astype(jnp.float32)  2.34 us
    ppermute x1, starting transfers between devices, per_device(): total = total + lax.ppermute(piece, 'tensor', pairs).astype(jnp.float32)  1.56 us
    ppermute x2, waiting for transfers between devices, to_inner(): lax.ppermute(values, 'expert', [(rank, rank ^ 1) for rank in range(expert...  1.06 us
  transfers between devices with their start and end apart: 10, of which 8 were waited for; matrix products, arithmetic and copies ran while one was open for 0% of the time, Pallas kernels for 7%

profile of v1, /device:TPU:0, one launch (start us, length us, event | category | flops | bytes accessed | tf_op | source)
XLA Modules:
  0.0 38.7 jit_solution(15246204810556895981)
XLA Ops:
  0.0 0.0 copy-start.2
  0.0 0.0 copy-start.3
  0.0 0.0 copy-start.4
  0.0 0.0 slice-start
  0.0 4.8 %shard_map.145 = (f32[8,2880]{1,0:T(8,128)S(1)}, bf16[8,2880]{1,0:T(8,128)(2,1)S(1)}) custom-call(s32[8]{0:T(128)} %lengths_hbm.1, bf16[8,16,64]{2,1,0:T(8,128)(2,1)} %queries_hbm.1, bf16[8,4,64]{2,1,0:T(4,128)(2,1)} %new_keys_hbm.1, bf16[8,4,64]{2,1,0:T(4,128)(2,1)} %new_values_hbm.1, bf16[8,256,256]{2,1,0:T(8,128)(2,1)} %bitcast.23, ...), custom_call_target="tpu_custom_call" | custom-call | flops 47185920 | bytes 7995392 | tf_op jit(solution)/shard_map/pallas_call | solution.py:212
  4.8 3.0 %collective-permute-start = (bf16[8,2880]{1,0:T(8,128)(2,1)S(1)}, bf16[8,2880]{1,0:T(8,128)(2,1)S(1)}, u32[]{:S(2)}, u32[]{:S(2)}) collective-permute-start(bf16[8,2880]{1,0:T(8,128)(2,1)S(1)} %get-tuple-element.20), channel_id=1, source_target_pairs={{0,1},{1,0},{2,3},{3,2},{4,5},{5,4},{6,7},{7,6},{8,9},{9,8},{10,11... | collective-permute-start | bytes 138248 | tf_op jit(solution)/shard_map/ppermute | solution.py:250
  7.9 0.0 copy-done.2
  7.9 0.0 copy-done.3
  7.9 0.0 copy-done.4
  7.9 0.0 slice-start.2
  8.0 0.1 select_reduce_fusion.weights_ref
  8.0 0.0 copy-start.1
  8.0 0.0 copy-start
  8.1 0.0 slice-start.1
  8.1 0.0 slice-start.3
  8.1 0.1 shard_map.146.table_ref
  8.2 0.7 %copy-done.1 = f32[2880]{0:T(1024)S(1)} copy-done((f32[2880]{0:T(1024)S(1)}, f32[2880]{0:T(1024)}, u32[]{:S(2)}) %copy-start.1) | copy-done | bytes 11544
  8.9 1.0 %collective-permute-done.received_ref = bf16[8,2880]{1,0:T(8,128)(2,1)S(1)} collective-permute-done((bf16[8,2880]{1,0:T(8,128)(2,1)S(1)}, bf16[8,2880]{1,0:T(8,128)(2,1)S(1)}, u32[]{:S(2)}, u32[]{:S(2)}) %collective-permute-start) | collective-permute-done | bytes 46112 | tf_op jit(solution)/shard_map/ppermute | solution.py:250
  9.9 0.0 copy-done
  9.9 0.1 shard_map.147
  10.1 4.2 %collective-permute-start.3 = (bf16[8,2944]{1,0:T(8,128)(2,1)S(1)}, bf16[8,2944]{1,0:T(8,128)(2,1)S(1)}, u32[]{:S(2)}, u32[]{:S(2)}) collective-permute-start(bf16[8,2944]{1,0:T(8,128)(2,1)S(1)} %get-tuple-element.22.refs_0_), channel_id=1, source_target_pairs={{0,12},{2,14},{4,8},{6,10},{8,4},{10,6},{12,0},{14,2},{1,13},{3,15... | collective-permute-start | bytes 141320 | tf_op jit(solution)/shard_map/ppermute | solution.py:395
  14.3 0.0 collective-permute-start.2
  14.3 0.6 %collective-permute-start.1 = (bf16[8,2944]{1,0:T(8,128)(2,1)S(1)}, bf16[8,2944]{1,0:T(8,128)(2,1)S(1)}, u32[]{:S(2)}, u32[]{:S(2)}) collective-permute-start(bf16[8,2944]{1,0:T(8,128)(2,1)S(1)} %get-tuple-element.22.refs_0_), channel_id=1, source_target_pairs={{0,4},{2,6},{4,0},{6,2},{8,12},{10,14},{12,8},{14,10},{1,5},{3,7},... | collective-permute-start | bytes 141320 | tf_op jit(solution)/shard_map/ppermute | solution.py:395
  14.9 1.4 %collective-permute-done.3.refs_3_ = bf16[8,2944]{1,0:T(8,128)(2,1)S(1)} collective-permute-done((bf16[8,2944]{1,0:T(8,128)(2,1)S(1)}, bf16[8,2944]{1,0:T(8,128)(2,1)S(1)}, u32[]{:S(2)}, u32[]{:S(2)}) %collective-permute-start.3) | collective-permute-done | bytes 47136 | tf_op jit(solution)/shard_map/ppermute | solution.py:395
  16.3 2.9 %collective-permute-done.2.refs_2_ = bf16[8,2944]{1,0:T(8,128)(2,1)S(1)} collective-permute-done((bf16[8,2944]{1,0:T(8,128)(2,1)S(1)}, bf16[8,2944]{1,0:T(8,128)(2,1)S(1)}, u32[]{:S(2)}, u32[]{:S(2)}) %collective-permute-start.2) | collective-permute-done | bytes 47136 | tf_op jit(solution)/shard_map/ppermute | solution.py:395
  19.2 0.0 collective-permute-done.1.refs_1_
  19.3 0.1 collective-permute-start.4
  19.3 0.0 slice-done
  19.3 0.0 slice-done.1
  19.4 0.0 slice-start.4
  19.4 0.5 %shard_map.150.refs_4_ = bf16[1,2880,208]{2,1,0:T(8,128)(2,1)S(1)} custom-call(bf16[1,720,2880]{2,1,0:T(8,128)(2,1)S(1)} %bitcast.15), custom_call_target="tpu_custom_call" | custom-call | flops 1 | bytes 1 | tf_op jit(solution)/shard_map/pallas_call | solution.py:54
  19.8 0.0 slice-done.2
  19.8 0.0 slice-done.3
  19.9 0.0 slice-start.5
  19.9 2.0 %shard_map.149 = (bf16[1,2880,720]{2,1,0:T(8,128)(2,1)S(1)}, bf16[1,2880,512]{2,1,0:T(8,128)(2,1)S(1)}) custom-call(bf16[1,720,2880]{2,1,0:T(8,128)(2,1)S(1)} %bitcast.19, bf16[1,720,2880]{2,1,0:T(8,128)(2,1)S(1)} %bitcast.16), custom_call_target="tpu_custom_call" | custom-call | flops 1 | bytes 1 | tf_op jit(solution)/shard_map/pallas_call | solution.py:54
  21.9 0.0 collective-permute-done.4.refs_1_
  21.9 0.0 slice-done.4
  21.9 0.0 slice-done.5
  21.9 2.4 %shard_map.151 = (f32[32,2880]{1,0:T(8,128)S(1)}, bf16[32,2880]{1,0:T(8,128)(2,1)S(1)}) custom-call(bf16[32,2944]{1,0:T(8,128)(2,1)S(1)} %shard_map.148.refs_0_, bf16[32,2944]{1,0:T(8,128)(2,1)S(1)} %collective-permute-done.4.refs_1_, bf16[1,2880,720]{2,1,0:T(8,128)(2,1)S(1)} %get-tuple-element.23.refs_2_, ...), custom_call_target="tpu_custom_call" | custom-call | flops 796262400 | bytes 12441600 | tf_op jit(solution)/shard_map/pallas_call | solution.py:54
  24.4 0.5 %collective-permute-start.5 = (bf16[32,2880]{1,0:T(8,128)(2,1)S(1)}, bf16[32,2880]{1,0:T(8,128)(2,1)S(1)}, u32[]{:S(2)}, u32[]{:S(2)}) collective-permute-start(bf16[32,2880]{1,0:T(8,128)(2,1)S(1)} %get-tuple-element.26), channel_id=1, source_target_pairs={{0,2},{2,0},{4,6},{6,4},{8,10},{10,8},{12,14},{14,12},{1,3},{3,1},... | collective-permute-start | bytes 552968 | tf_op jit(solution)/shard_map/ppermute | solution.py:398
  24.9 1.1 %collective-permute-done.5.received_ref = bf16[32,2880]{1,0:T(8,128)(2,1)S(1)} collective-permute-done((bf16[32,2880]{1,0:T(8,128)(2,1)S(1)}, bf16[32,2880]{1,0:T(8,128)(2,1)S(1)}, u32[]{:S(2)}, u32[]{:S(2)}) %collective-permute-start.5) | collective-permute-done | bytes 184352 | tf_op jit(solution)/shard_map/ppermute | solution.py:398
  26.0 0.2 collective-permute-start.6
  26.2 2.0 %collective-permute-start.7 = (bf16[8,2880]{1,0:T(8,128)(2,1)S(1)}, bf16[8,2880]{1,0:T(8,128)(2,1)S(1)}, u32[]{:S(2)}, u32[]{:S(2)}) collective-permute-start(bf16[8,2880]{1,0:T(8,128)(2,1)S(1)} %get-tuple-element.29), channel_id=1, source_target_pairs={{0,8},{2,10},{4,12},{6,14},{8,0},{10,2},{12,4},{14,6},{1,9},{3,11}... | collective-permute-start | bytes 138248 | tf_op jit(solution)/shard_map/ppermute | solution.py:395
  28.2 2.3 %collective-permute-start.8 = (bf16[8,2880]{1,0:T(8,128)(2,1)S(1)}, bf16[8,2880]{1,0:T(8,128)(2,1)S(1)}, u32[]{:S(2)}, u32[]{:S(2)}) collective-permute-start(bf16[8,2880]{1,0:T(8,128)(2,1)S(1)} %get-tuple-element.30), channel_id=1, source_target_pairs={{0,12},{2,14},{4,8},{6,10},{8,4},{10,6},{12,0},{14,2},{1,13},{3,15... | collective-permute-start | bytes 138248 | tf_op jit(solution)/shard_map/ppermute | solution.py:395
  30.5 0.2 collective-permute-done.6.refs_1_
  30.6 0.5 %collective-permute-done.7.refs_2_ = bf16[8,2880]{1,0:T(8,128)(2,1)S(1)} collective-permute-done((bf16[8,2880]{1,0:T(8,128)(2,1)S(1)}, bf16[8,2880]{1,0:T(8,128)(2,1)S(1)}, u32[]{:S(2)}, u32[]{:S(2)}) %collective-permute-start.7) | collective-permute-done | bytes 46112 | tf_op jit(solution)/shard_map/ppermute | solution.py:395
  31.2 2.9 %collective-permute-done.8.refs_3_ = bf16[8,2880]{1,0:T(8,128)(2,1)S(1)} collective-permute-done((bf16[8,2880]{1,0:T(8,128)(2,1)S(1)}, bf16[8,2880]{1,0:T(8,128)(2,1)S(1)}, u32[]{:S(2)}, u32[]{:S(2)}) %collective-permute-start.8) | collective-permute-done | bytes 46112 | tf_op jit(solution)/shard_map/ppermute | solution.py:395
  34.0 0.2 shard_map.153
  34.2 1.6 %collective-permute-start.9 = (bf16[8,1440]{1,0:T(8,128)(2,1)S(1)}, bf16[8,1440]{1,0:T(8,128)(2,1)S(1)}, u32[]{:S(2)}, u32[]{:S(2)}) collective-permute-start(bf16[8,1440]{1,0:T(8,128)(2,1)S(1)} %get-tuple-element.32), channel_id=1, source_target_pairs={{0,1},{1,0},{2,3},{3,2},{4,5},{5,4},{6,7},{7,6},{8,9},{9,8},{10,11... | collective-permute-start | bytes 69128 | tf_op jit(solution)/shard_map/ppermute | solution.py:474
  35.8 2.3 %collective-permute-done.9 = bf16[8,1440]{1,0:T(8,128)(2,1)S(1)} collective-permute-done((bf16[8,1440]{1,0:T(8,128)(2,1)S(1)}, bf16[8,1440]{1,0:T(8,128)(2,1)S(1)}, u32[]{:S(2)}, u32[]{:S(2)}) %collective-permute-start.9) | collective-permute-done | bytes 23072 | tf_op jit(solution)/shard_map/ppermute | solution.py:474
  38.1 0.6 %add_convert_fusion = bf16[8,1440]{1,0:T(8,128)(2,1)} fusion(f32[8,1440]{1,0:T(8,128)S(1)} %get-tuple-element.31, bf16[8,1440]{1,0:T(8,128)(2,1)S(1)} %collective-permute-done.9), kind=kLoop, calls=%fused_computation | loop fusion | flops 34560 | bytes 92160 | tf_op jit(solution)/shard_map/convert_element_type | solution.py:475
  (9 shorter events, 0.1 us)
Async XLA Ops:
  0.0 7.9 %copy-start.2 = (f32[8,4]{0,1:T(4,128)S(1)}, f32[8,4]{0,1:T(4,128)}, u32[]{:S(2)}) copy-start(f32[8,4]{0,1:T(4,128)} %param.25) | copy-start | bytes 388
  0.0 7.9 %copy-start.3 = (s32[8,4]{0,1:T(4,128)S(1)}, s32[8,4]{0,1:T(4,128)}, u32[]{:S(2)}) copy-start(s32[8,4]{0,1:T(4,128)} %param.26) | copy-start | bytes 388
  0.0 7.9 %copy-start.4 = (s32[8,4]{0,1:T(4,128)S(1)}, s32[8,4]{0,1:T(4,128)}, u32[]{:S(2)}) copy-start(s32[8,4]{0,1:T(4,128)} %param.24) | copy-start | bytes 388
  0.0 19.3 %slice-start = ((s8[4239360]{0:T(1024)(128)(4,1)}), s8[45056]{0:T(1024)(128)(4,1)S(1)}, s32[]{:S(2)}) async-start(s8[4239360]{0:T(1024)(128)(4,1)} %bitcast.13), calls=%async_computation | async-start | bytes 90112
  4.8 5.1 %collective-permute-start = (bf16[8,2880]{1,0:T(8,128)(2,1)S(1)}, bf16[8,2880]{1,0:T(8,128)(2,1)S(1)}, u32[]{:S(2)}, u32[]{:S(2)}) collective-permute-start(bf16[8,2880]{1,0:T(8,128)(2,1)S(1)} %get-tuple-element.20), channel_id=1, source_target_pairs={{0,1},{1,0},{2,3},{3,2},{4,5},{5,4},{6,7},{7,6},{8,9},{9,8},{10,11... | collective-permute-start | bytes 138248 | tf_op jit(solution)/shard_map/ppermute | solution.py:250
  7.9 11.9 %slice-start.2 = ((s8[4239360]{0:T(1024)(128)(4,1)}), s8[4194304]{0:T(1024)(128)(4,1)S(1)}, s32[]{:S(2)}) async-start(s8[4239360]{0:T(1024)(128)(4,1)} %bitcast.17), calls=%async_computation.2 | async-start | bytes 8388608
  8.0 0.9 %copy-start.1 = (f32[2880]{0:T(1024)S(1)}, f32[2880]{0:T(1024)}, u32[]{:S(2)}) copy-start(f32[2880]{0:T(1024)} %param.23) | copy-start | bytes 34564
  8.0 1.9 %copy-start = (bf16[8,2880]{1,0:T(8,128)(2,1)S(1)}, bf16[8,2880]{1,0:T(8,128)(2,1)}, u32[]{:S(2)}) copy-start(bf16[8,2880]{1,0:T(8,128)(2,1)} %hidden_ref.1) | copy-start | bytes 138244
  8.1 11.3 %slice-start.1 = ((s8[4239360]{0:T(1024)(128)(4,1)}), s8[4194304]{0:T(1024)(128)(4,1)S(1)}, s32[]{:S(2)}) async-start(s8[4239360]{0:T(1024)(128)(4,1)} %bitcast.13), calls=%async_computation.1 | async-start | bytes 8388608
  8.1 11.8 %slice-start.3 = ((s8[4239360]{0:T(1024)(128)(4,1)}), s8[45056]{0:T(1024)(128)(4,1)S(1)}, s32[]{:S(2)}) async-start(s8[4239360]{0:T(1024)(128)(4,1)} %bitcast.17), calls=%async_computation.3 | async-start | bytes 90112
  10.1 6.2 %collective-permute-start.3 = (bf16[8,2944]{1,0:T(8,128)(2,1)S(1)}, bf16[8,2944]{1,0:T(8,128)(2,1)S(1)}, u32[]{:S(2)}, u32[]{:S(2)}) collective-permute-start(bf16[8,2944]{1,0:T(8,128)(2,1)S(1)} %get-tuple-element.22.refs_0_), channel_id=1, source_target_pairs={{0,12},{2,14},{4,8},{6,10},{8,4},{10,6},{12,0},{14,2},{1,13},{3,15... | collective-permute-start | bytes 141320 | tf_op jit(solution)/shard_map/ppermute | solution.py:395
  14.3 5.0 %collective-permute-start.2 = (bf16[8,2944]{1,0:T(8,128)(2,1)S(1)}, bf16[8,2944]{1,0:T(8,128)(2,1)S(1)}, u32[]{:S(2)}, u32[]{:S(2)}) collective-permute-start(bf16[8,2944]{1,0:T(8,128)(2,1)S(1)} %get-tuple-element.22.refs_0_), channel_id=1, source_target_pairs={{0,8},{2,10},{4,12},{6,14},{8,0},{10,2},{12,4},{14,6},{1,9},{3,11}... | collective-permute-start | bytes 141320 | tf_op jit(solution)/shard_map/ppermute | solution.py:395
  14.3 5.0 %collective-permute-start.1 = (bf16[8,2944]{1,0:T(8,128)(2,1)S(1)}, bf16[8,2944]{1,0:T(8,128)(2,1)S(1)}, u32[]{:S(2)}, u32[]{:S(2)}) collective-permute-start(bf16[8,2944]{1,0:T(8,128)(2,1)S(1)} %get-tuple-element.22.refs_0_), channel_id=1, source_target_pairs={{0,4},{2,6},{4,0},{6,2},{8,12},{10,14},{12,8},{14,10},{1,5},{3,7},... | collective-permute-start | bytes 141320 | tf_op jit(solution)/shard_map/ppermute | solution.py:395
  19.3 2.7 %collective-permute-start.4 = (bf16[32,2944]{1,0:T(8,128)(2,1)S(1)}, bf16[32,2944]{1,0:T(8,128)(2,1)S(1)}, u32[]{:S(2)}, u32[]{:S(2)}) collective-permute-start(bf16[32,2944]{1,0:T(8,128)(2,1)S(1)} %shard_map.148.refs_0_), channel_id=1, source_target_pairs={{0,2},{2,0},{4,6},{6,4},{8,10},{10,8},{12,14},{14,12},{1,3},{3,1},... | collective-permute-start | bytes 565256 | tf_op jit(solution)/shard_map/ppermute | solution.py:398
  19.4 2.6 %slice-start.4 = ((s8[4239360]{0:T(1024)(128)(4,1)}), s8[4194304]{0:T(1024)(128)(4,1)S(1)}, s32[]{:S(2)}) async-start(s8[4239360]{0:T(1024)(128)(4,1)} %bitcast.20), calls=%async_computation.4 | async-start | bytes 8388608
  19.9 2.1 %slice-start.5 = ((s8[4239360]{0:T(1024)(128)(4,1)}), s8[45056]{0:T(1024)(128)(4,1)S(1)}, s32[]{:S(2)}) async-start(s8[4239360]{0:T(1024)(128)(4,1)} %bitcast.20), calls=%async_computation.5 | async-start | bytes 90112
  24.4 1.6 %collective-permute-start.5 = (bf16[32,2880]{1,0:T(8,128)(2,1)S(1)}, bf16[32,2880]{1,0:T(8,128)(2,1)S(1)}, u32[]{:S(2)}, u32[]{:S(2)}) collective-permute-start(bf16[32,2880]{1,0:T(8,128)(2,1)S(1)} %get-tuple-element.26), channel_id=1, source_target_pairs={{0,2},{2,0},{4,6},{6,4},{8,10},{10,8},{12,14},{14,12},{1,3},{3,1},... | collective-permute-start | bytes 552968 | tf_op jit(solution)/shard_map/ppermute | solution.py:398
  26.0 4.6 %collective-permute-start.6 = (bf16[8,2880]{1,0:T(8,128)(2,1)S(1)}, bf16[8,2880]{1,0:T(8,128)(2,1)S(1)}, u32[]{:S(2)}, u32[]{:S(2)}) collective-permute-start(bf16[8,2880]{1,0:T(8,128)(2,1)S(1)} %get-tuple-element.28), channel_id=1, source_target_pairs={{0,4},{2,6},{4,0},{6,2},{8,12},{10,14},{12,8},{14,10},{1,5},{3,7},... | collective-permute-start | bytes 138248 | tf_op jit(solution)/shard_map/ppermute | solution.py:395
  26.2 5.0 %collective-permute-start.7 = (bf16[8,2880]{1,0:T(8,128)(2,1)S(1)}, bf16[8,2880]{1,0:T(8,128)(2,1)S(1)}, u32[]{:S(2)}, u32[]{:S(2)}) collective-permute-start(bf16[8,2880]{1,0:T(8,128)(2,1)S(1)} %get-tuple-element.29), channel_id=1, source_target_pairs={{0,8},{2,10},{4,12},{6,14},{8,0},{10,2},{12,4},{14,6},{1,9},{3,11}... | collective-permute-start | bytes 138248 | tf_op jit(solution)/shard_map/ppermute | solution.py:395
  28.2 5.9 %collective-permute-start.8 = (bf16[8,2880]{1,0:T(8,128)(2,1)S(1)}, bf16[8,2880]{1,0:T(8,128)(2,1)S(1)}, u32[]{:S(2)}, u32[]{:S(2)}) collective-permute-start(bf16[8,2880]{1,0:T(8,128)(2,1)S(1)} %get-tuple-element.30), channel_id=1, source_target_pairs={{0,12},{2,14},{4,8},{6,10},{8,4},{10,6},{12,0},{14,2},{1,13},{3,15... | collective-permute-start | bytes 138248 | tf_op jit(solution)/shard_map/ppermute | solution.py:395
  34.2 3.9 %collective-permute-start.9 = (bf16[8,1440]{1,0:T(8,128)(2,1)S(1)}, bf16[8,1440]{1,0:T(8,128)(2,1)S(1)}, u32[]{:S(2)}, u32[]{:S(2)}) collective-permute-start(bf16[8,1440]{1,0:T(8,128)(2,1)S(1)} %get-tuple-element.32), channel_id=1, source_target_pairs={{0,1},{1,0},{2,3},{3,2},{4,5},{5,4},{6,7},{7,6},{8,9},{9,8},{10,11... | collective-permute-start | bytes 69128 | tf_op jit(solution)/shard_map/ppermute | solution.py:474

commit v2 on v1

--- a/solution.py
+++ b/solution.py
@@ -316,16 +316,11 @@
         expert = lax.axis_index("expert") * local_experts + local
         chosen = (column == expert) | (column == expert + experts)
         weight = jnp.sum(jnp.where(chosen, table, 0.0), axis=1, keepdims=True)
-        part = None
-        start = 0
-        for up_ref in (first_ref, second_ref):
-            piece = pl.ds(start, up_ref.shape[2])
-            gate = mm(rows, gate_ref[local, :, piece])
-            up = mm(rows, up_ref[local])
-            active = (gate * jax.nn.sigmoid(GLU_SLOPE * gate) * (up + 1.0)).astype(jnp.bfloat16)
-            term = mm(active, down_ref[local, piece])
-            part = term if part is None else part + term
-            start += up_ref.shape[2]
+        gate = mm(rows, gate_ref[local])
+        up = [mm(rows, up_ref[local]) for up_ref in (first_ref, second_ref)]
+        up = jnp.concatenate(up, axis=1)
+        active = (gate * jax.nn.sigmoid(GLU_SLOPE * gate) * (up + 1.0)).astype(jnp.bfloat16)
+        part = mm(active, down_ref[local])
         part = part * weight
         total = part if total is None else total + part
     half = mine_ref.shape[0]
@@ -361,6 +356,14 @@
     base_ref[...] = slab_of(total + residual_ref[...], rank)
     for step, sent_ref in enumerate(sent_refs, 1):
         sent_ref[...] = slab_of(total, rank ^ step).astype(jnp.bfloat16)
+
+
+def output_kernel(base_ref, *refs):
+    *received_refs, output_ref = refs
+    total = base_ref[...]
+    for received_ref in received_refs:
+        total = total + received_ref[...].astype(jnp.float32)
+    output_ref[...] = total.astype(jnp.bfloat16)
 
 
 def per_device(
@@ -469,10 +472,19 @@
         moved=half[0] * width * 2,
         limit=2 * MIB,
     )
+    arrived = []
     for step, piece in enumerate(sent, 1):
         pairs = [(rank, rank ^ step) for rank in range(tensor_ranks)]
-        total = total + lax.ppermute(piece, "tensor", pairs).astype(jnp.float32)
-    return total.astype(jnp.bfloat16)
+        arrived.append(lax.ppermute(piece, "tensor", pairs))
+    (output,) = call(
+        output_kernel,
+        [(slab, jnp.bfloat16)],
+        (total, *arrived),
+        flops=slab[0] * slab[1] * tensor_ranks,
+        moved=slab[0] * slab[1] * 2,
+        limit=2 * MIB,
+    )
+    return output
 
 
 def solution(mesh):

time: 38.9 us -> 38.8 us (level)
  other arithmetic: 0.72 us -> 0.11 us
  Pallas kernels: 10.1 us -> 10.7 us
    convert_element_type x1 -> x0, other arithmetic: 0.62 us -> none  [per_device(): return total.astype(jnp.bfloat16)]
    pallas_call x8 -> x9, Pallas kernels: 5.33 us -> 5.86 us  [call(): pl.pallas_call(kernel, out_shape=[jax.ShapeDtypeStruct(shape, dtype) for...]
  transfers between devices with their start and end apart: 10 -> 10, of which waited for: 8 -> 7; matrix products, arithmetic and copies ran while one was open for 0% -> 0% of each run, Pallas kernels for 7% -> 7%
where the time goes in v2:
time: 38.8 us; the launch traced here: 38.6 us
  starting transfers between devices  14.5 us (37%)
  waiting for transfers between devices  12.3 us (32%)
  Pallas kernels  10.7 us (28%)
  local copies, waits for them, and re-layouts  0.81 us (2%)
    ppermute x6, starting transfers between devices, to_outer(): return lax.ppermute(values, 'expert', pairs)  9.29 us
    ppermute x6, waiting for transfers between devices, to_outer(): return lax.ppermute(values, 'expert', pairs)  7.91 us
    pallas_call x9, Pallas kernels, call(): pl.pallas_call(kernel, out_shape=[jax.ShapeDtypeStruct(shape, dtype) for...  5.86 us
    pallas_call x1, Pallas kernels, attend_and_project(): pl.pallas_call(functools.partial(attend_kernel, pieces), out_shape=[jax.S...  4.82 us
    ppermute x1, starting transfers between devices, exchange(): received = lax.ppermute(sent, axis, pairs)  3.05 us
    ppermute x1, waiting for transfers between devices, per_device(): arrived.append(lax.ppermute(piece, 'tensor', pairs))  2.34 us
    ppermute x1, starting transfers between devices, per_device(): arrived.append(lax.ppermute(piece, 'tensor', pairs))  1.56 us
    ppermute x2, waiting for transfers between devices, to_inner(): lax.ppermute(values, 'expert', [(rank, rank ^ 1) for rank in range(expert...  1.06 us
  transfers between devices with their start and end apart: 10, of which 7 were waited for; matrix products, arithmetic and copies ran while one was open for 0% of the time, Pallas kernels for 7%

profile of v2, /device:TPU:0, one launch (start us, length us, event | category | flops | bytes accessed | tf_op | source)
XLA Modules:
  0.0 38.6 jit_solution(16786131682817684047)
XLA Ops:
  0.0 0.0 copy-start.2
  0.0 0.0 copy-start.3
  0.0 0.0 copy-start.4
  0.0 0.0 slice-start
  0.0 4.8 %shard_map.145 = (f32[8,2880]{1,0:T(8,128)S(1)}, bf16[8,2880]{1,0:T(8,128)(2,1)S(1)}) custom-call(s32[8]{0:T(128)} %lengths_hbm.1, bf16[8,16,64]{2,1,0:T(8,128)(2,1)} %queries_hbm.1, bf16[8,4,64]{2,1,0:T(4,128)(2,1)} %new_keys_hbm.1, bf16[8,4,64]{2,1,0:T(4,128)(2,1)} %new_values_hbm.1, bf16[8,256,256]{2,1,0:T(8,128)(2,1)} %bitcast.23, ...), custom_call_target="tpu_custom_call" | custom-call | flops 47185920 | bytes 7995392 | tf_op jit(solution)/shard_map/pallas_call | solution.py:212
  4.8 3.0 %collective-permute-start = (bf16[8,2880]{1,0:T(8,128)(2,1)S(1)}, bf16[8,2880]{1,0:T(8,128)(2,1)S(1)}, u32[]{:S(2)}, u32[]{:S(2)}) collective-permute-start(bf16[8,2880]{1,0:T(8,128)(2,1)S(1)} %get-tuple-element.20), channel_id=1, source_target_pairs={{0,1},{1,0},{2,3},{3,2},{4,5},{5,4},{6,7},{7,6},{8,9},{9,8},{10,11... | collective-permute-start | bytes 138248 | tf_op jit(solution)/shard_map/ppermute | solution.py:250
  7.9 0.0 copy-done.2
  7.9 0.0 copy-done.3
  7.9 0.0 copy-done.4
  7.9 0.0 slice-start.2
  8.0 0.1 select_reduce_fusion.weights_ref
  8.0 0.0 copy-start.1
  8.0 0.0 copy-start
  8.1 0.0 slice-start.1
  8.1 0.0 slice-start.3
  8.1 0.1 shard_map.146.table_ref
  8.2 0.7 %copy-done.1 = f32[2880]{0:T(1024)S(1)} copy-done((f32[2880]{0:T(1024)S(1)}, f32[2880]{0:T(1024)}, u32[]{:S(2)}) %copy-start.1) | copy-done | bytes 11544
  8.9 1.0 %collective-permute-done.received_ref = bf16[8,2880]{1,0:T(8,128)(2,1)S(1)} collective-permute-done((bf16[8,2880]{1,0:T(8,128)(2,1)S(1)}, bf16[8,2880]{1,0:T(8,128)(2,1)S(1)}, u32[]{:S(2)}, u32[]{:S(2)}) %collective-permute-start) | collective-permute-done | bytes 46112 | tf_op jit(solution)/shard_map/ppermute | solution.py:250
  9.9 0.0 copy-done
  9.9 0.1 shard_map.147
  10.1 4.2 %collective-permute-start.3 = (bf16[8,2944]{1,0:T(8,128)(2,1)S(1)}, bf16[8,2944]{1,0:T(8,128)(2,1)S(1)}, u32[]{:S(2)}, u32[]{:S(2)}) collective-permute-start(bf16[8,2944]{1,0:T(8,128)(2,1)S(1)} %get-tuple-element.22.refs_0_), channel_id=1, source_target_pairs={{0,12},{2,14},{4,8},{6,10},{8,4},{10,6},{12,0},{14,2},{1,13},{3,15... | collective-permute-start | bytes 141320 | tf_op jit(solution)/shard_map/ppermute | solution.py:398
  14.3 0.0 collective-permute-start.2
  14.3 0.6 %collective-permute-start.1 = (bf16[8,2944]{1,0:T(8,128)(2,1)S(1)}, bf16[8,2944]{1,0:T(8,128)(2,1)S(1)}, u32[]{:S(2)}, u32[]{:S(2)}) collective-permute-start(bf16[8,2944]{1,0:T(8,128)(2,1)S(1)} %get-tuple-element.22.refs_0_), channel_id=1, source_target_pairs={{0,4},{2,6},{4,0},{6,2},{8,12},{10,14},{12,8},{14,10},{1,5},{3,7},... | collective-permute-start | bytes 141320 | tf_op jit(solution)/shard_map/ppermute | solution.py:398
  14.9 1.4 %collective-permute-done.3.refs_3_ = bf16[8,2944]{1,0:T(8,128)(2,1)S(1)} collective-permute-done((bf16[8,2944]{1,0:T(8,128)(2,1)S(1)}, bf16[8,2944]{1,0:T(8,128)(2,1)S(1)}, u32[]{:S(2)}, u32[]{:S(2)}) %collective-permute-start.3) | collective-permute-done | bytes 47136 | tf_op jit(solution)/shard_map/ppermute | solution.py:398
  16.3 2.9 %collective-permute-done.2.refs_2_ = bf16[8,2944]{1,0:T(8,128)(2,1)S(1)} collective-permute-done((bf16[8,2944]{1,0:T(8,128)(2,1)S(1)}, bf16[8,2944]{1,0:T(8,128)(2,1)S(1)}, u32[]{:S(2)}, u32[]{:S(2)}) %collective-permute-start.2) | collective-permute-done | bytes 47136 | tf_op jit(solution)/shard_map/ppermute | solution.py:398
  19.2 0.0 collective-permute-done.1.refs_1_
  19.3 0.1 collective-permute-start.4
  19.3 0.0 slice-done
  19.3 0.0 slice-done.1
  19.4 0.0 slice-start.4
  19.4 0.5 %shard_map.150.refs_4_ = bf16[1,2880,208]{2,1,0:T(8,128)(2,1)S(1)} custom-call(bf16[1,720,2880]{2,1,0:T(8,128)(2,1)S(1)} %bitcast.15), custom_call_target="tpu_custom_call" | custom-call | flops 1 | bytes 1 | tf_op jit(solution)/shard_map/pallas_call | solution.py:54
  19.8 0.0 slice-done.2
  19.8 0.0 slice-done.3
  19.9 0.0 slice-start.5
  19.9 2.0 %shard_map.149 = (bf16[1,2880,720]{2,1,0:T(8,128)(2,1)S(1)}, bf16[1,2880,512]{2,1,0:T(8,128)(2,1)S(1)}) custom-call(bf16[1,720,2880]{2,1,0:T(8,128)(2,1)S(1)} %bitcast.19, bf16[1,720,2880]{2,1,0:T(8,128)(2,1)S(1)} %bitcast.16), custom_call_target="tpu_custom_call" | custom-call | flops 1 | bytes 1 | tf_op jit(solution)/shard_map/pallas_call | solution.py:54
  21.9 0.0 collective-permute-done.4.refs_1_
  21.9 0.0 slice-done.4
  21.9 0.0 slice-done.5
  21.9 2.3 %shard_map.151 = (f32[32,2880]{1,0:T(8,128)S(1)}, bf16[32,2880]{1,0:T(8,128)(2,1)S(1)}) custom-call(bf16[32,2944]{1,0:T(8,128)(2,1)S(1)} %shard_map.148.refs_0_, bf16[32,2944]{1,0:T(8,128)(2,1)S(1)} %collective-permute-done.4.refs_1_, bf16[1,2880,720]{2,1,0:T(8,128)(2,1)S(1)} %get-tuple-element.23.refs_2_, ...), custom_call_target="tpu_custom_call" | custom-call | flops 796262400 | bytes 12441600 | tf_op jit(solution)/shard_map/pallas_call | solution.py:54
  24.3 0.5 %collective-permute-start.5 = (bf16[32,2880]{1,0:T(8,128)(2,1)S(1)}, bf16[32,2880]{1,0:T(8,128)(2,1)S(1)}, u32[]{:S(2)}, u32[]{:S(2)}) collective-permute-start(bf16[32,2880]{1,0:T(8,128)(2,1)S(1)} %get-tuple-element.26), channel_id=1, source_target_pairs={{0,2},{2,0},{4,6},{6,4},{8,10},{10,8},{12,14},{14,12},{1,3},{3,1},... | collective-permute-start | bytes 552968 | tf_op jit(solution)/shard_map/ppermute | solution.py:401
  24.8 1.1 %collective-permute-done.5.received_ref = bf16[32,2880]{1,0:T(8,128)(2,1)S(1)} collective-permute-done((bf16[32,2880]{1,0:T(8,128)(2,1)S(1)}, bf16[32,2880]{1,0:T(8,128)(2,1)S(1)}, u32[]{:S(2)}, u32[]{:S(2)}) %collective-permute-start.5) | collective-permute-done | bytes 184352 | tf_op jit(solution)/shard_map/ppermute | solution.py:401
  25.9 0.2 collective-permute-start.6
  26.1 2.0 %collective-permute-start.7 = (bf16[8,2880]{1,0:T(8,128)(2,1)S(1)}, bf16[8,2880]{1,0:T(8,128)(2,1)S(1)}, u32[]{:S(2)}, u32[]{:S(2)}) collective-permute-start(bf16[8,2880]{1,0:T(8,128)(2,1)S(1)} %get-tuple-element.29), channel_id=1, source_target_pairs={{0,8},{2,10},{4,12},{6,14},{8,0},{10,2},{12,4},{14,6},{1,9},{3,11}... | collective-permute-start | bytes 138248 | tf_op jit(solution)/shard_map/ppermute | solution.py:398
  28.1 2.3 %collective-permute-start.8 = (bf16[8,2880]{1,0:T(8,128)(2,1)S(1)}, bf16[8,2880]{1,0:T(8,128)(2,1)S(1)}, u32[]{:S(2)}, u32[]{:S(2)}) collective-permute-start(bf16[8,2880]{1,0:T(8,128)(2,1)S(1)} %get-tuple-element.30), channel_id=1, source_target_pairs={{0,12},{2,14},{4,8},{6,10},{8,4},{10,6},{12,0},{14,2},{1,13},{3,15... | collective-permute-start | bytes 138248 | tf_op jit(solution)/shard_map/ppermute | solution.py:398
  30.4 0.7 %collective-permute-done.6.refs_1_ = bf16[8,2880]{1,0:T(8,128)(2,1)S(1)} collective-permute-done((bf16[8,2880]{1,0:T(8,128)(2,1)S(1)}, bf16[8,2880]{1,0:T(8,128)(2,1)S(1)}, u32[]{:S(2)}, u32[]{:S(2)}) %collective-permute-start.6) | collective-permute-done | bytes 46112 | tf_op jit(solution)/shard_map/ppermute | solution.py:398
  31.0 0.0 collective-permute-done.7.refs_2_
  31.1 2.9 %collective-permute-done.8.refs_3_ = bf16[8,2880]{1,0:T(8,128)(2,1)S(1)} collective-permute-done((bf16[8,2880]{1,0:T(8,128)(2,1)S(1)}, bf16[8,2880]{1,0:T(8,128)(2,1)S(1)}, u32[]{:S(2)}, u32[]{:S(2)}) %collective-permute-start.8) | collective-permute-done | bytes 46112 | tf_op jit(solution)/shard_map/ppermute | solution.py:398
  34.0 0.2 shard_map.153
  34.1 1.6 %collective-permute-start.9 = (bf16[8,1440]{1,0:T(8,128)(2,1)S(1)}, bf16[8,1440]{1,0:T(8,128)(2,1)S(1)}, u32[]{:S(2)}, u32[]{:S(2)}) collective-permute-start(bf16[8,1440]{1,0:T(8,128)(2,1)S(1)} %get-tuple-element.32), channel_id=1, source_target_pairs={{0,1},{1,0},{2,3},{3,2},{4,5},{5,4},{6,7},{7,6},{8,9},{9,8},{10,11... | collective-permute-start | bytes 69128 | tf_op jit(solution)/shard_map/ppermute | solution.py:478
  35.7 2.3 %collective-permute-done.9.refs_0_ = bf16[8,1440]{1,0:T(8,128)(2,1)S(1)} collective-permute-done((bf16[8,1440]{1,0:T(8,128)(2,1)S(1)}, bf16[8,1440]{1,0:T(8,128)(2,1)S(1)}, u32[]{:S(2)}, u32[]{:S(2)}) %collective-permute-start.9) | collective-permute-done | bytes 23072 | tf_op jit(solution)/shard_map/ppermute | solution.py:478
  38.0 0.6 %shard_map.154 = bf16[8,1440]{1,0:T(8,128)(2,1)} custom-call(f32[8,1440]{1,0:T(8,128)S(1)} %get-tuple-element.31.base_ref, bf16[8,1440]{1,0:T(8,128)(2,1)S(1)} %collective-permute-done.9.refs_0_), custom_call_target="tpu_custom_call" | custom-call | flops 23040 | bytes 23040 | tf_op jit(solution)/shard_map/pallas_call | solution.py:54
  (9 shorter events, 0.1 us)
Async XLA Ops:
  0.0 7.9 %copy-start.2 = (f32[8,4]{0,1:T(4,128)S(1)}, f32[8,4]{0,1:T(4,128)}, u32[]{:S(2)}) copy-start(f32[8,4]{0,1:T(4,128)} %param.25) | copy-start | bytes 388
  0.0 7.9 %copy-start.3 = (s32[8,4]{0,1:T(4,128)S(1)}, s32[8,4]{0,1:T(4,128)}, u32[]{:S(2)}) copy-start(s32[8,4]{0,1:T(4,128)} %param.26) | copy-start | bytes 388
  0.0 7.9 %copy-start.4 = (s32[8,4]{0,1:T(4,128)S(1)}, s32[8,4]{0,1:T(4,128)}, u32[]{:S(2)}) copy-start(s32[8,4]{0,1:T(4,128)} %param.24) | copy-start | bytes 388
  0.0 19.3 %slice-start = ((s8[4239360]{0:T(1024)(128)(4,1)}), s8[45056]{0:T(1024)(128)(4,1)S(1)}, s32[]{:S(2)}) async-start(s8[4239360]{0:T(1024)(128)(4,1)} %bitcast.13), calls=%async_computation | async-start | bytes 90112
  4.8 5.1 %collective-permute-start = (bf16[8,2880]{1,0:T(8,128)(2,1)S(1)}, bf16[8,2880]{1,0:T(8,128)(2,1)S(1)}, u32[]{:S(2)}, u32[]{:S(2)}) collective-permute-start(bf16[8,2880]{1,0:T(8,128)(2,1)S(1)} %get-tuple-element.20), channel_id=1, source_target_pairs={{0,1},{1,0},{2,3},{3,2},{4,5},{5,4},{6,7},{7,6},{8,9},{9,8},{10,11... | collective-permute-start | bytes 138248 | tf_op jit(solution)/shard_map/ppermute | solution.py:250
  7.9 11.9 %slice-start.2 = ((s8[4239360]{0:T(1024)(128)(4,1)}), s8[4194304]{0:T(1024)(128)(4,1)S(1)}, s32[]{:S(2)}) async-start(s8[4239360]{0:T(1024)(128)(4,1)} %bitcast.17), calls=%async_computation.2 | async-start | bytes 8388608
  8.0 0.9 %copy-start.1 = (f32[2880]{0:T(1024)S(1)}, f32[2880]{0:T(1024)}, u32[]{:S(2)}) copy-start(f32[2880]{0:T(1024)} %param.23) | copy-start | bytes 34564
  8.0 1.9 %copy-start = (bf16[8,2880]{1,0:T(8,128)(2,1)S(1)}, bf16[8,2880]{1,0:T(8,128)(2,1)}, u32[]{:S(2)}) copy-start(bf16[8,2880]{1,0:T(8,128)(2,1)} %hidden_ref.1) | copy-start | bytes 138244
  8.1 11.3 %slice-start.1 = ((s8[4239360]{0:T(1024)(128)(4,1)}), s8[4194304]{0:T(1024)(128)(4,1)S(1)}, s32[]{:S(2)}) async-start(s8[4239360]{0:T(1024)(128)(4,1)} %bitcast.13), calls=%async_computation.1 | async-start | bytes 8388608
  8.1 11.8 %slice-start.3 = ((s8[4239360]{0:T(1024)(128)(4,1)}), s8[45056]{0:T(1024)(128)(4,1)S(1)}, s32[]{:S(2)}) async-start(s8[4239360]{0:T(1024)(128)(4,1)} %bitcast.17), calls=%async_computation.3 | async-start | bytes 90112
  10.1 6.2 %collective-permute-start.3 = (bf16[8,2944]{1,0:T(8,128)(2,1)S(1)}, bf16[8,2944]{1,0:T(8,128)(2,1)S(1)}, u32[]{:S(2)}, u32[]{:S(2)}) collective-permute-start(bf16[8,2944]{1,0:T(8,128)(2,1)S(1)} %get-tuple-element.22.refs_0_), channel_id=1, source_target_pairs={{0,12},{2,14},{4,8},{6,10},{8,4},{10,6},{12,0},{14,2},{1,13},{3,15... | collective-permute-start | bytes 141320 | tf_op jit(solution)/shard_map/ppermute | solution.py:398
  14.3 5.0 %collective-permute-start.2 = (bf16[8,2944]{1,0:T(8,128)(2,1)S(1)}, bf16[8,2944]{1,0:T(8,128)(2,1)S(1)}, u32[]{:S(2)}, u32[]{:S(2)}) collective-permute-start(bf16[8,2944]{1,0:T(8,128)(2,1)S(1)} %get-tuple-element.22.refs_0_), channel_id=1, source_target_pairs={{0,8},{2,10},{4,12},{6,14},{8,0},{10,2},{12,4},{14,6},{1,9},{3,11}... | collective-permute-start | bytes 141320 | tf_op jit(solution)/shard_map/ppermute | solution.py:398
  14.3 5.0 %collective-permute-start.1 = (bf16[8,2944]{1,0:T(8,128)(2,1)S(1)}, bf16[8,2944]{1,0:T(8,128)(2,1)S(1)}, u32[]{:S(2)}, u32[]{:S(2)}) collective-permute-start(bf16[8,2944]{1,0:T(8,128)(2,1)S(1)} %get-tuple-element.22.refs_0_), channel_id=1, source_target_pairs={{0,4},{2,6},{4,0},{6,2},{8,12},{10,14},{12,8},{14,10},{1,5},{3,7},... | collective-permute-start | bytes 141320 | tf_op jit(solution)/shard_map/ppermute | solution.py:398
  19.3 2.7 %collective-permute-start.4 = (bf16[32,2944]{1,0:T(8,128)(2,1)S(1)}, bf16[32,2944]{1,0:T(8,128)(2,1)S(1)}, u32[]{:S(2)}, u32[]{:S(2)}) collective-permute-start(bf16[32,2944]{1,0:T(8,128)(2,1)S(1)} %shard_map.148.refs_0_), channel_id=1, source_target_pairs={{0,2},{2,0},{4,6},{6,4},{8,10},{10,8},{12,14},{14,12},{1,3},{3,1},... | collective-permute-start | bytes 565256 | tf_op jit(solution)/shard_map/ppermute | solution.py:401
  19.4 2.6 %slice-start.4 = ((s8[4239360]{0:T(1024)(128)(4,1)}), s8[4194304]{0:T(1024)(128)(4,1)S(1)}, s32[]{:S(2)}) async-start(s8[4239360]{0:T(1024)(128)(4,1)} %bitcast.20), calls=%async_computation.4 | async-start | bytes 8388608
  19.9 2.1 %slice-start.5 = ((s8[4239360]{0:T(1024)(128)(4,1)}), s8[45056]{0:T(1024)(128)(4,1)S(1)}, s32[]{:S(2)}) async-start(s8[4239360]{0:T(1024)(128)(4,1)} %bitcast.20), calls=%async_computation.5 | async-start | bytes 90112
  24.3 1.6 %collective-permute-start.5 = (bf16[32,2880]{1,0:T(8,128)(2,1)S(1)}, bf16[32,2880]{1,0:T(8,128)(2,1)S(1)}, u32[]{:S(2)}, u32[]{:S(2)}) collective-permute-start(bf16[32,2880]{1,0:T(8,128)(2,1)S(1)} %get-tuple-element.26), channel_id=1, source_target_pairs={{0,2},{2,0},{4,6},{6,4},{8,10},{10,8},{12,14},{14,12},{1,3},{3,1},... | collective-permute-start | bytes 552968 | tf_op jit(solution)/shard_map/ppermute | solution.py:401
  25.9 5.1 %collective-permute-start.6 = (bf16[8,2880]{1,0:T(8,128)(2,1)S(1)}, bf16[8,2880]{1,0:T(8,128)(2,1)S(1)}, u32[]{:S(2)}, u32[]{:S(2)}) collective-permute-start(bf16[8,2880]{1,0:T(8,128)(2,1)S(1)} %get-tuple-element.28), channel_id=1, source_target_pairs={{0,4},{2,6},{4,0},{6,2},{8,12},{10,14},{12,8},{14,10},{1,5},{3,7},... | collective-permute-start | bytes 138248 | tf_op jit(solution)/shard_map/ppermute | solution.py:398
  26.1 5.0 %collective-permute-start.7 = (bf16[8,2880]{1,0:T(8,128)(2,1)S(1)}, bf16[8,2880]{1,0:T(8,128)(2,1)S(1)}, u32[]{:S(2)}, u32[]{:S(2)}) collective-permute-start(bf16[8,2880]{1,0:T(8,128)(2,1)S(1)} %get-tuple-element.29), channel_id=1, source_target_pairs={{0,8},{2,10},{4,12},{6,14},{8,0},{10,2},{12,4},{14,6},{1,9},{3,11}... | collective-permute-start | bytes 138248 | tf_op jit(solution)/shard_map/ppermute | solution.py:398
  28.1 5.9 %collective-permute-start.8 = (bf16[8,2880]{1,0:T(8,128)(2,1)S(1)}, bf16[8,2880]{1,0:T(8,128)(2,1)S(1)}, u32[]{:S(2)}, u32[]{:S(2)}) collective-permute-start(bf16[8,2880]{1,0:T(8,128)(2,1)S(1)} %get-tuple-element.30), channel_id=1, source_target_pairs={{0,12},{2,14},{4,8},{6,10},{8,4},{10,6},{12,0},{14,2},{1,13},{3,15... | collective-permute-start | bytes 138248 | tf_op jit(solution)/shard_map/ppermute | solution.py:398
  34.1 3.9 %collective-permute-start.9 = (bf16[8,1440]{1,0:T(8,128)(2,1)S(1)}, bf16[8,1440]{1,0:T(8,128)(2,1)S(1)}, u32[]{:S(2)}, u32[]{:S(2)}) collective-permute-start(bf16[8,1440]{1,0:T(8,128)(2,1)S(1)} %get-tuple-element.32), channel_id=1, source_target_pairs={{0,1},{1,0},{2,3},{3,2},{4,5},{5,4},{6,7},{7,6},{8,9},{9,8},{10,11... | collective-permute-start | bytes 69128 | tf_op jit(solution)/shard_map/ppermute | solution.py:478

commit v3 on v1

--- a/solution.py
+++ b/solution.py
@@ -316,16 +316,11 @@
         expert = lax.axis_index("expert") * local_experts + local
         chosen = (column == expert) | (column == expert + experts)
         weight = jnp.sum(jnp.where(chosen, table, 0.0), axis=1, keepdims=True)
-        part = None
-        start = 0
-        for up_ref in (first_ref, second_ref):
-            piece = pl.ds(start, up_ref.shape[2])
-            gate = mm(rows, gate_ref[local, :, piece])
-            up = mm(rows, up_ref[local])
-            active = (gate * jax.nn.sigmoid(GLU_SLOPE * gate) * (up + 1.0)).astype(jnp.bfloat16)
-            term = mm(active, down_ref[local, piece])
-            part = term if part is None else part + term
-            start += up_ref.shape[2]
+        gate = mm(rows, gate_ref[local])
+        up = [mm(rows, up_ref[local]) for up_ref in (first_ref, second_ref)]
+        up = jnp.concatenate(up, axis=1)
+        active = (gate * jax.nn.sigmoid(GLU_SLOPE * gate) * (up + 1.0)).astype(jnp.bfloat16)
+        part = mm(active, down_ref[local])
         part = part * weight
         total = part if total is None else total + part
     half = mine_ref.shape[0]
@@ -387,7 +382,7 @@
     experts = local_experts * expert_ranks
     inner = 2
     outer = expert_ranks // inner
-    cut = 3 * hidden_units // 4 // 128 * 128
+    cut = -(-hidden_units // 256) * 128
     row_width = -(-(width + 2 * experts) // 128) * 128
 
     def to_outer(values, step):

time: 38.9 us -> 38.9 us (level)
  no operation moved by 1% of the time
where the time goes in v3:
time: 38.9 us; the launch traced here: 38.8 us
  starting transfers between devices  14.5 us (37%)
  waiting for transfers between devices  12.3 us (32%)
  Pallas kernels  10.2 us (26%)
  local copies, waits for them, and re-layouts  0.81 us (2%)
  other arithmetic  0.72 us (2%)
    ppermute x6, starting transfers between devices, to_outer(): return lax.ppermute(values, 'expert', pairs)  9.29 us
    ppermute x6, waiting for transfers between devices, to_outer(): return lax.ppermute(values, 'expert', pairs)  7.91 us
    pallas_call x8, Pallas kernels, call(): pl.pallas_call(kernel, out_shape=[jax.ShapeDtypeStruct(shape, dtype) for...  5.39 us
    pallas_call x1, Pallas kernels, attend_and_project(): pl.pallas_call(functools.partial(attend_kernel, pieces), out_shape=[jax.S...  4.82 us
    ppermute x1, starting transfers between devices, exchange(): received = lax.ppermute(sent, axis, pairs)  3.05 us
    ppermute x1, waiting for transfers between devices, per_device(): total = total + lax.ppermute(piece, 'tensor', pairs).astype(jnp.float32)  2.34 us
    ppermute x1, starting transfers between devices, per_device(): total = total + lax.ppermute(piece, 'tensor', pairs).astype(jnp.float32)  1.55 us
    ppermute x2, waiting for transfers between devices, to_inner(): lax.ppermute(values, 'expert', [(rank, rank ^ 1) for rank in range(expert...  1.06 us
  transfers between devices with their start and end apart: 10, of which 8 were waited for; matrix products, arithmetic and copies ran while one was open for 0% of the time, Pallas kernels for 7%

profile of v3, /device:TPU:0, one launch (start us, length us, event | category | flops | bytes accessed | tf_op | source)
XLA Modules:
  0.0 38.8 jit_solution(3025599172132727493)
XLA Ops:
  0.0 0.0 copy-start.2
  0.0 0.0 copy-start.3
  0.0 0.0 copy-start.4
  0.0 0.0 slice-start
  0.0 4.8 %shard_map.145 = (f32[8,2880]{1,0:T(8,128)S(1)}, bf16[8,2880]{1,0:T(8,128)(2,1)S(1)}) custom-call(s32[8]{0:T(128)} %lengths_hbm.1, bf16[8,16,64]{2,1,0:T(8,128)(2,1)} %queries_hbm.1, bf16[8,4,64]{2,1,0:T(4,128)(2,1)} %new_keys_hbm.1, bf16[8,4,64]{2,1,0:T(4,128)(2,1)} %new_values_hbm.1, bf16[8,256,256]{2,1,0:T(8,128)(2,1)} %bitcast.23, ...), custom_call_target="tpu_custom_call" | custom-call | flops 47185920 | bytes 7995392 | tf_op jit(solution)/shard_map/pallas_call | solution.py:212
  4.8 3.0 %collective-permute-start = (bf16[8,2880]{1,0:T(8,128)(2,1)S(1)}, bf16[8,2880]{1,0:T(8,128)(2,1)S(1)}, u32[]{:S(2)}, u32[]{:S(2)}) collective-permute-start(bf16[8,2880]{1,0:T(8,128)(2,1)S(1)} %get-tuple-element.20), channel_id=1, source_target_pairs={{0,1},{1,0},{2,3},{3,2},{4,5},{5,4},{6,7},{7,6},{8,9},{9,8},{10,11... | collective-permute-start | bytes 138248 | tf_op jit(solution)/shard_map/ppermute | solution.py:250
  7.9 0.0 copy-done.2
  7.9 0.0 copy-done.3
  7.9 0.0 copy-done.4
  7.9 0.0 slice-start.2
  8.0 0.1 select_reduce_fusion.weights_ref
  8.0 0.0 copy-start.1
  8.0 0.0 copy-start
  8.1 0.0 slice-start.1
  8.1 0.0 slice-start.3
  8.1 0.1 shard_map.146.table_ref
  8.2 0.7 %copy-done.1 = f32[2880]{0:T(1024)S(1)} copy-done((f32[2880]{0:T(1024)S(1)}, f32[2880]{0:T(1024)}, u32[]{:S(2)}) %copy-start.1) | copy-done | bytes 11544
  8.9 1.0 %collective-permute-done.received_ref = bf16[8,2880]{1,0:T(8,128)(2,1)S(1)} collective-permute-done((bf16[8,2880]{1,0:T(8,128)(2,1)S(1)}, bf16[8,2880]{1,0:T(8,128)(2,1)S(1)}, u32[]{:S(2)}, u32[]{:S(2)}) %collective-permute-start) | collective-permute-done | bytes 46112 | tf_op jit(solution)/shard_map/ppermute | solution.py:250
  9.9 0.0 copy-done
  9.9 0.1 shard_map.147
  10.1 4.2 %collective-permute-start.3 = (bf16[8,2944]{1,0:T(8,128)(2,1)S(1)}, bf16[8,2944]{1,0:T(8,128)(2,1)S(1)}, u32[]{:S(2)}, u32[]{:S(2)}) collective-permute-start(bf16[8,2944]{1,0:T(8,128)(2,1)S(1)} %get-tuple-element.22.refs_0_), channel_id=1, source_target_pairs={{0,12},{2,14},{4,8},{6,10},{8,4},{10,6},{12,0},{14,2},{1,13},{3,15... | collective-permute-start | bytes 141320 | tf_op jit(solution)/shard_map/ppermute | solution.py:390
  14.3 0.0 collective-permute-start.2
  14.3 0.6 %collective-permute-start.1 = (bf16[8,2944]{1,0:T(8,128)(2,1)S(1)}, bf16[8,2944]{1,0:T(8,128)(2,1)S(1)}, u32[]{:S(2)}, u32[]{:S(2)}) collective-permute-start(bf16[8,2944]{1,0:T(8,128)(2,1)S(1)} %get-tuple-element.22.refs_0_), channel_id=1, source_target_pairs={{0,4},{2,6},{4,0},{6,2},{8,12},{10,14},{12,8},{14,10},{1,5},{3,7},... | collective-permute-start | bytes 141320 | tf_op jit(solution)/shard_map/ppermute | solution.py:390
  14.9 1.4 %collective-permute-done.3.refs_3_ = bf16[8,2944]{1,0:T(8,128)(2,1)S(1)} collective-permute-done((bf16[8,2944]{1,0:T(8,128)(2,1)S(1)}, bf16[8,2944]{1,0:T(8,128)(2,1)S(1)}, u32[]{:S(2)}, u32[]{:S(2)}) %collective-permute-start.3) | collective-permute-done | bytes 47136 | tf_op jit(solution)/shard_map/ppermute | solution.py:390
  16.3 2.9 %collective-permute-done.2.refs_2_ = bf16[8,2944]{1,0:T(8,128)(2,1)S(1)} collective-permute-done((bf16[8,2944]{1,0:T(8,128)(2,1)S(1)}, bf16[8,2944]{1,0:T(8,128)(2,1)S(1)}, u32[]{:S(2)}, u32[]{:S(2)}) %collective-permute-start.2) | collective-permute-done | bytes 47136 | tf_op jit(solution)/shard_map/ppermute | solution.py:390
  19.2 0.0 collective-permute-done.1.refs_1_
  19.3 0.1 collective-permute-start.4
  19.3 0.0 slice-done
  19.3 0.0 slice-done.1
  19.4 0.0 slice-start.4
  19.4 0.7 %shard_map.150.refs_4_ = bf16[1,2880,336]{2,1,0:T(8,128)(2,1)S(1)} custom-call(bf16[1,720,2880]{2,1,0:T(8,128)(2,1)S(1)} %bitcast.15), custom_call_target="tpu_custom_call" | custom-call | flops 1 | bytes 1 | tf_op jit(solution)/shard_map/pallas_call | solution.py:54
  20.0 0.0 slice-done.2
  20.0 0.0 slice-done.3
  20.1 0.0 slice-start.5
  20.1 1.8 %shard_map.149 = (bf16[1,2880,720]{2,1,0:T(8,128)(2,1)S(1)}, bf16[1,2880,384]{2,1,0:T(8,128)(2,1)S(1)}) custom-call(bf16[1,720,2880]{2,1,0:T(8,128)(2,1)S(1)} %bitcast.19, bf16[1,720,2880]{2,1,0:T(8,128)(2,1)S(1)} %bitcast.16), custom_call_target="tpu_custom_call" | custom-call | flops 1 | bytes 1 | tf_op jit(solution)/shard_map/pallas_call | solution.py:54
  21.9 0.0 collective-permute-done.4.refs_1_
  21.9 0.0 slice-done.4
  21.9 0.0 slice-done.5
  21.9 2.5 %shard_map.151 = (f32[32,2880]{1,0:T(8,128)S(1)}, bf16[32,2880]{1,0:T(8,128)(2,1)S(1)}) custom-call(bf16[32,2944]{1,0:T(8,128)(2,1)S(1)} %shard_map.148.refs_0_, bf16[32,2944]{1,0:T(8,128)(2,1)S(1)} %collective-permute-done.4.refs_1_, bf16[1,2880,720]{2,1,0:T(8,128)(2,1)S(1)} %get-tuple-element.23.refs_2_, ...), custom_call_target="tpu_custom_call" | custom-call | flops 796262400 | bytes 12441600 | tf_op jit(solution)/shard_map/pallas_call | solution.py:54
  24.4 0.5 %collective-permute-start.5 = (bf16[32,2880]{1,0:T(8,128)(2,1)S(1)}, bf16[32,2880]{1,0:T(8,128)(2,1)S(1)}, u32[]{:S(2)}, u32[]{:S(2)}) collective-permute-start(bf16[32,2880]{1,0:T(8,128)(2,1)S(1)} %get-tuple-element.26), channel_id=1, source_target_pairs={{0,2},{2,0},{4,6},{6,4},{8,10},{10,8},{12,14},{14,12},{1,3},{3,1},... | collective-permute-start | bytes 552968 | tf_op jit(solution)/shard_map/ppermute | solution.py:393
  25.0 1.1 %collective-permute-done.5.received_ref = bf16[32,2880]{1,0:T(8,128)(2,1)S(1)} collective-permute-done((bf16[32,2880]{1,0:T(8,128)(2,1)S(1)}, bf16[32,2880]{1,0:T(8,128)(2,1)S(1)}, u32[]{:S(2)}, u32[]{:S(2)}) %collective-permute-start.5) | collective-permute-done | bytes 184352 | tf_op jit(solution)/shard_map/ppermute | solution.py:393
  26.1 0.2 collective-permute-start.6
  26.2 2.0 %collective-permute-start.7 = (bf16[8,2880]{1,0:T(8,128)(2,1)S(1)}, bf16[8,2880]{1,0:T(8,128)(2,1)S(1)}, u32[]{:S(2)}, u32[]{:S(2)}) collective-permute-start(bf16[8,2880]{1,0:T(8,128)(2,1)S(1)} %get-tuple-element.29), channel_id=1, source_target_pairs={{0,8},{2,10},{4,12},{6,14},{8,0},{10,2},{12,4},{14,6},{1,9},{3,11}... | collective-permute-start | bytes 138248 | tf_op jit(solution)/shard_map/ppermute | solution.py:390
  28.2 2.3 %collective-permute-start.8 = (bf16[8,2880]{1,0:T(8,128)(2,1)S(1)}, bf16[8,2880]{1,0:T(8,128)(2,1)S(1)}, u32[]{:S(2)}, u32[]{:S(2)}) collective-permute-start(bf16[8,2880]{1,0:T(8,128)(2,1)S(1)} %get-tuple-element.30), channel_id=1, source_target_pairs={{0,12},{2,14},{4,8},{6,10},{8,4},{10,6},{12,0},{14,2},{1,13},{3,15... | collective-permute-start | bytes 138248 | tf_op jit(solution)/shard_map/ppermute | solution.py:390
  30.5 0.2 collective-permute-done.6.refs_1_
  30.7 0.5 %collective-permute-done.7.refs_2_ = bf16[8,2880]{1,0:T(8,128)(2,1)S(1)} collective-permute-done((bf16[8,2880]{1,0:T(8,128)(2,1)S(1)}, bf16[8,2880]{1,0:T(8,128)(2,1)S(1)}, u32[]{:S(2)}, u32[]{:S(2)}) %collective-permute-start.7) | collective-permute-done | bytes 46112 | tf_op jit(solution)/shard_map/ppermute | solution.py:390
  31.2 2.9 %collective-permute-done.8.refs_3_ = bf16[8,2880]{1,0:T(8,128)(2,1)S(1)} collective-permute-done((bf16[8,2880]{1,0:T(8,128)(2,1)S(1)}, bf16[8,2880]{1,0:T(8,128)(2,1)S(1)}, u32[]{:S(2)}, u32[]{:S(2)}) %collective-permute-start.8) | collective-permute-done | bytes 46112 | tf_op jit(solution)/shard_map/ppermute | solution.py:390
  34.1 0.2 shard_map.153
  34.3 1.6 %collective-permute-start.9 = (bf16[8,1440]{1,0:T(8,128)(2,1)S(1)}, bf16[8,1440]{1,0:T(8,128)(2,1)S(1)}, u32[]{:S(2)}, u32[]{:S(2)}) collective-permute-start(bf16[8,1440]{1,0:T(8,128)(2,1)S(1)} %get-tuple-element.32), channel_id=1, source_target_pairs={{0,1},{1,0},{2,3},{3,2},{4,5},{5,4},{6,7},{7,6},{8,9},{9,8},{10,11... | collective-permute-start | bytes 69128 | tf_op jit(solution)/shard_map/ppermute | solution.py:469
  35.8 2.3 %collective-permute-done.9 = bf16[8,1440]{1,0:T(8,128)(2,1)S(1)} collective-permute-done((bf16[8,1440]{1,0:T(8,128)(2,1)S(1)}, bf16[8,1440]{1,0:T(8,128)(2,1)S(1)}, u32[]{:S(2)}, u32[]{:S(2)}) %collective-permute-start.9) | collective-permute-done | bytes 23072 | tf_op jit(solution)/shard_map/ppermute | solution.py:469
  38.2 0.6 %add_convert_fusion = bf16[8,1440]{1,0:T(8,128)(2,1)} fusion(f32[8,1440]{1,0:T(8,128)S(1)} %get-tuple-element.31, bf16[8,1440]{1,0:T(8,128)(2,1)S(1)} %collective-permute-done.9), kind=kLoop, calls=%fused_computation | loop fusion | flops 34560 | bytes 92160 | tf_op jit(solution)/shard_map/convert_element_type | solution.py:470
  (9 shorter events, 0.1 us)
Async XLA Ops:
  0.0 7.9 %copy-start.2 = (f32[8,4]{0,1:T(4,128)S(1)}, f32[8,4]{0,1:T(4,128)}, u32[]{:S(2)}) copy-start(f32[8,4]{0,1:T(4,128)} %param.25) | copy-start | bytes 388
  0.0 7.9 %copy-start.3 = (s32[8,4]{0,1:T(4,128)S(1)}, s32[8,4]{0,1:T(4,128)}, u32[]{:S(2)}) copy-start(s32[8,4]{0,1:T(4,128)} %param.26) | copy-start | bytes 388
  0.0 7.9 %copy-start.4 = (s32[8,4]{0,1:T(4,128)S(1)}, s32[8,4]{0,1:T(4,128)}, u32[]{:S(2)}) copy-start(s32[8,4]{0,1:T(4,128)} %param.24) | copy-start | bytes 388
  0.0 19.3 %slice-start = ((s8[4239360]{0:T(1024)(128)(4,1)}), s8[45056]{0:T(1024)(128)(4,1)S(1)}, s32[]{:S(2)}) async-start(s8[4239360]{0:T(1024)(128)(4,1)} %bitcast.13), calls=%async_computation | async-start | bytes 90112
  4.8 5.1 %collective-permute-start = (bf16[8,2880]{1,0:T(8,128)(2,1)S(1)}, bf16[8,2880]{1,0:T(8,128)(2,1)S(1)}, u32[]{:S(2)}, u32[]{:S(2)}) collective-permute-start(bf16[8,2880]{1,0:T(8,128)(2,1)S(1)} %get-tuple-element.20), channel_id=1, source_target_pairs={{0,1},{1,0},{2,3},{3,2},{4,5},{5,4},{6,7},{7,6},{8,9},{9,8},{10,11... | collective-permute-start | bytes 138248 | tf_op jit(solution)/shard_map/ppermute | solution.py:250
  7.9 12.1 %slice-start.2 = ((s8[4239360]{0:T(1024)(128)(4,1)}), s8[4194304]{0:T(1024)(128)(4,1)S(1)}, s32[]{:S(2)}) async-start(s8[4239360]{0:T(1024)(128)(4,1)} %bitcast.17), calls=%async_computation.2 | async-start | bytes 8388608
  8.0 0.9 %copy-start.1 = (f32[2880]{0:T(1024)S(1)}, f32[2880]{0:T(1024)}, u32[]{:S(2)}) copy-start(f32[2880]{0:T(1024)} %param.23) | copy-start | bytes 34564
  8.0 1.9 %copy-start = (bf16[8,2880]{1,0:T(8,128)(2,1)S(1)}, bf16[8,2880]{1,0:T(8,128)(2,1)}, u32[]{:S(2)}) copy-start(bf16[8,2880]{1,0:T(8,128)(2,1)} %hidden_ref.1) | copy-start | bytes 138244
  8.1 11.3 %slice-start.1 = ((s8[4239360]{0:T(1024)(128)(4,1)}), s8[4194304]{0:T(1024)(128)(4,1)S(1)}, s32[]{:S(2)}) async-start(s8[4239360]{0:T(1024)(128)(4,1)} %bitcast.13), calls=%async_computation.1 | async-start | bytes 8388608
  8.1 12.0 %slice-start.3 = ((s8[4239360]{0:T(1024)(128)(4,1)}), s8[45056]{0:T(1024)(128)(4,1)S(1)}, s32[]{:S(2)}) async-start(s8[4239360]{0:T(1024)(128)(4,1)} %bitcast.17), calls=%async_computation.3 | async-start | bytes 90112
  10.1 6.2 %collective-permute-start.3 = (bf16[8,2944]{1,0:T(8,128)(2,1)S(1)}, bf16[8,2944]{1,0:T(8,128)(2,1)S(1)}, u32[]{:S(2)}, u32[]{:S(2)}) collective-permute-start(bf16[8,2944]{1,0:T(8,128)(2,1)S(1)} %get-tuple-element.22.refs_0_), channel_id=1, source_target_pairs={{0,12},{2,14},{4,8},{6,10},{8,4},{10,6},{12,0},{14,2},{1,13},{3,15... | collective-permute-start | bytes 141320 | tf_op jit(solution)/shard_map/ppermute | solution.py:390
  14.3 5.0 %collective-permute-start.2 = (bf16[8,2944]{1,0:T(8,128)(2,1)S(1)}, bf16[8,2944]{1,0:T(8,128)(2,1)S(1)}, u32[]{:S(2)}, u32[]{:S(2)}) collective-permute-start(bf16[8,2944]{1,0:T(8,128)(2,1)S(1)} %get-tuple-element.22.refs_0_), channel_id=1, source_target_pairs={{0,8},{2,10},{4,12},{6,14},{8,0},{10,2},{12,4},{14,6},{1,9},{3,11}... | collective-permute-start | bytes 141320 | tf_op jit(solution)/shard_map/ppermute | solution.py:390
  14.3 5.0 %collective-permute-start.1 = (bf16[8,2944]{1,0:T(8,128)(2,1)S(1)}, bf16[8,2944]{1,0:T(8,128)(2,1)S(1)}, u32[]{:S(2)}, u32[]{:S(2)}) collective-permute-start(bf16[8,2944]{1,0:T(8,128)(2,1)S(1)} %get-tuple-element.22.refs_0_), channel_id=1, source_target_pairs={{0,4},{2,6},{4,0},{6,2},{8,12},{10,14},{12,8},{14,10},{1,5},{3,7},... | collective-permute-start | bytes 141320 | tf_op jit(solution)/shard_map/ppermute | solution.py:390
  19.3 2.7 %collective-permute-start.4 = (bf16[32,2944]{1,0:T(8,128)(2,1)S(1)}, bf16[32,2944]{1,0:T(8,128)(2,1)S(1)}, u32[]{:S(2)}, u32[]{:S(2)}) collective-permute-start(bf16[32,2944]{1,0:T(8,128)(2,1)S(1)} %shard_map.148.refs_0_), channel_id=1, source_target_pairs={{0,2},{2,0},{4,6},{6,4},{8,10},{10,8},{12,14},{14,12},{1,3},{3,1},... | collective-permute-start | bytes 565256 | tf_op jit(solution)/shard_map/ppermute | solution.py:393
  19.4 2.6 %slice-start.4 = ((s8[4239360]{0:T(1024)(128)(4,1)}), s8[4194304]{0:T(1024)(128)(4,1)S(1)}, s32[]{:S(2)}) async-start(s8[4239360]{0:T(1024)(128)(4,1)} %bitcast.20), calls=%async_computation.4 | async-start | bytes 8388608
  20.1 1.9 %slice-start.5 = ((s8[4239360]{0:T(1024)(128)(4,1)}), s8[45056]{0:T(1024)(128)(4,1)S(1)}, s32[]{:S(2)}) async-start(s8[4239360]{0:T(1024)(128)(4,1)} %bitcast.20), calls=%async_computation.5 | async-start | bytes 90112
  24.4 1.6 %collective-permute-start.5 = (bf16[32,2880]{1,0:T(8,128)(2,1)S(1)}, bf16[32,2880]{1,0:T(8,128)(2,1)S(1)}, u32[]{:S(2)}, u32[]{:S(2)}) collective-permute-start(bf16[32,2880]{1,0:T(8,128)(2,1)S(1)} %get-tuple-element.26), channel_id=1, source_target_pairs={{0,2},{2,0},{4,6},{6,4},{8,10},{10,8},{12,14},{14,12},{1,3},{3,1},... | collective-permute-start | bytes 552968 | tf_op jit(solution)/shard_map/ppermute | solution.py:393
  26.1 4.6 %collective-permute-start.6 = (bf16[8,2880]{1,0:T(8,128)(2,1)S(1)}, bf16[8,2880]{1,0:T(8,128)(2,1)S(1)}, u32[]{:S(2)}, u32[]{:S(2)}) collective-permute-start(bf16[8,2880]{1,0:T(8,128)(2,1)S(1)} %get-tuple-element.28), channel_id=1, source_target_pairs={{0,4},{2,6},{4,0},{6,2},{8,12},{10,14},{12,8},{14,10},{1,5},{3,7},... | collective-permute-start | bytes 138248 | tf_op jit(solution)/shard_map/ppermute | solution.py:390
  26.2 5.0 %collective-permute-start.7 = (bf16[8,2880]{1,0:T(8,128)(2,1)S(1)}, bf16[8,2880]{1,0:T(8,128)(2,1)S(1)}, u32[]{:S(2)}, u32[]{:S(2)}) collective-permute-start(bf16[8,2880]{1,0:T(8,128)(2,1)S(1)} %get-tuple-element.29), channel_id=1, source_target_pairs={{0,8},{2,10},{4,12},{6,14},{8,0},{10,2},{12,4},{14,6},{1,9},{3,11}... | collective-permute-start | bytes 138248 | tf_op jit(solution)/shard_map/ppermute | solution.py:390
  28.2 5.9 %collective-permute-start.8 = (bf16[8,2880]{1,0:T(8,128)(2,1)S(1)}, bf16[8,2880]{1,0:T(8,128)(2,1)S(1)}, u32[]{:S(2)}, u32[]{:S(2)}) collective-permute-start(bf16[8,2880]{1,0:T(8,128)(2,1)S(1)} %get-tuple-element.30), channel_id=1, source_target_pairs={{0,12},{2,14},{4,8},{6,10},{8,4},{10,6},{12,0},{14,2},{1,13},{3,15... | collective-permute-start | bytes 138248 | tf_op jit(solution)/shard_map/ppermute | solution.py:390
  34.3 3.9 %collective-permute-start.9 = (bf16[8,1440]{1,0:T(8,128)(2,1)S(1)}, bf16[8,1440]{1,0:T(8,128)(2,1)S(1)}, u32[]{:S(2)}, u32[]{:S(2)}) collective-permute-start(bf16[8,1440]{1,0:T(8,128)(2,1)S(1)} %get-tuple-element.32), channel_id=1, source_target_pairs={{0,1},{1,0},{2,3},{3,2},{4,5},{5,4},{6,7},{7,6},{8,9},{9,8},{10,11... | collective-permute-start | bytes 69128 | tf_op jit(solution)/shard_map/ppermute | solution.py:469

commit v4 on v3

--- a/solution.py
+++ b/solution.py
@@ -137,6 +137,17 @@
         * scaling
     )
 
+    repeat = (iota((span, lanes), 0) % head_dim == iota((span, lanes), 1) % head_dim).astype(
+        jnp.bfloat16
+    )
+    own_lanes = iota((rows, lanes), 1) // head_dim == iota((rows, lanes), 0) % group
+    sums = (kv_heads * sequences, rows)
+    chosen = (iota(sums, 0) % sequences == iota(sums, 1) // heads) & (
+        iota(sums, 0) // sequences == iota(sums, 1) % heads // group
+    )
+    chosen = chosen.astype(jnp.bfloat16)
+    own_wide = mm(own_values, spread).astype(jnp.bfloat16)
+
     copies[4].wait()
     slots = keys_ref.shape[2]
     scores = []
@@ -153,7 +164,7 @@
     cache_prob = (cache_exp / totals).astype(jnp.bfloat16)
     own_prob = own_exp / totals
     own_prob = jnp.where(own_pair, own_prob, 0.0).astype(jnp.bfloat16)
-    own_part = mm(own_prob, mm(own_values, spread).astype(jnp.bfloat16))
+    own_part = mm(own_prob, own_wide)
 
     copies[5].wait()
     attended = [
@@ -166,16 +177,8 @@
     ]
     attended = jnp.concatenate(attended, axis=0) + own_part
     attended = jnp.where(same_head, attended, 0.0).astype(jnp.bfloat16)
-    repeat = (iota((span, lanes), 0) % head_dim == iota((span, lanes), 1) % head_dim).astype(
-        jnp.bfloat16
-    )
-    own_lanes = iota((rows, lanes), 1) // head_dim == iota((rows, lanes), 0) % group
     placed = jnp.where(own_lanes, mm(attended, repeat), 0.0).astype(jnp.bfloat16)
-    sums = (kv_heads * sequences, rows)
-    chosen = (iota(sums, 0) % sequences == iota(sums, 1) // heads) & (
-        iota(sums, 0) // sequences == iota(sums, 1) % heads // group
-    )
-    by_head = mm(chosen.astype(jnp.bfloat16), placed)
+    by_head = mm(chosen, placed)
     for head in range(kv_heads):
         attended_ref[:, head * lanes : (head + 1) * lanes] = by_head[
             head * sequences : (head + 1) * sequences
@@ -382,7 +385,7 @@
     experts = local_experts * expert_ranks
     inner = 2
     outer = expert_ranks // inner
-    cut = -(-hidden_units // 256) * 128
+    cut = 3 * hidden_units // 4 // 128 * 128
     row_width = -(-(width + 2 * experts) // 128) * 128
 
     def to_outer(values, step):

time: 38.9 us -> 38.8 us (level)
  transfers between devices with their start and end apart: 10 -> 10, of which waited for: 8 -> 7; matrix products, arithmetic and copies ran while one was open for 0% -> 0% of each run, Pallas kernels for 7% -> 7%
where the time goes in v4:
time: 38.8 us; the launch traced here: 38.6 us
  starting transfers between devices  14.5 us (37%)
  waiting for transfers between devices  12.3 us (32%)
  Pallas kernels  10.1 us (26%)
  local copies, waits for them, and re-layouts  0.81 us (2%)
  other arithmetic  0.72 us (2%)
    ppermute x6, starting transfers between devices, to_outer(): return lax.ppermute(values, 'expert', pairs)  9.29 us
    ppermute x6, waiting for transfers between devices, to_outer(): return lax.ppermute(values, 'expert', pairs)  7.91 us
    pallas_call x8, Pallas kernels, call(): pl.pallas_call(kernel, out_shape=[jax.ShapeDtypeStruct(shape, dtype) for...  5.24 us
    pallas_call x1, Pallas kernels, attend_and_project(): pl.pallas_call(functools.partial(attend_kernel, pieces), out_shape=[jax.S...  4.82 us
    ppermute x1, starting transfers between devices, exchange(): received = lax.ppermute(sent, axis, pairs)  3.05 us
    ppermute x1, waiting for transfers between devices, per_device(): total = total + lax.ppermute(piece, 'tensor', pairs).astype(jnp.float32)  2.34 us
    ppermute x1, starting transfers between devices, per_device(): total = total + lax.ppermute(piece, 'tensor', pairs).astype(jnp.float32)  1.56 us
    ppermute x2, waiting for transfers between devices, to_inner(): lax.ppermute(values, 'expert', [(rank, rank ^ 1) for rank in range(expert...  1.06 us
  transfers between devices with their start and end apart: 10, of which 7 were waited for; matrix products, arithmetic and copies ran while one was open for 0% of the time, Pallas kernels for 7%

profile of v4, /device:TPU:0, one launch (start us, length us, event | category | flops | bytes accessed | tf_op | source)
XLA Modules:
  0.0 38.6 jit_solution(10759451469231112987)
XLA Ops:
  0.0 0.0 copy-start.2
  0.0 0.0 copy-start.3
  0.0 0.0 copy-start.4
  0.0 0.0 slice-start
  0.0 4.8 %shard_map.145 = (f32[8,2880]{1,0:T(8,128)S(1)}, bf16[8,2880]{1,0:T(8,128)(2,1)S(1)}) custom-call(s32[8]{0:T(128)} %lengths_hbm.1, bf16[8,16,64]{2,1,0:T(8,128)(2,1)} %queries_hbm.1, bf16[8,4,64]{2,1,0:T(4,128)(2,1)} %new_keys_hbm.1, bf16[8,4,64]{2,1,0:T(4,128)(2,1)} %new_values_hbm.1, bf16[8,256,256]{2,1,0:T(8,128)(2,1)} %bitcast.23, ...), custom_call_target="tpu_custom_call" | custom-call | flops 47185920 | bytes 7995392 | tf_op jit(solution)/shard_map/pallas_call | solution.py:215
  4.8 3.0 %collective-permute-start = (bf16[8,2880]{1,0:T(8,128)(2,1)S(1)}, bf16[8,2880]{1,0:T(8,128)(2,1)S(1)}, u32[]{:S(2)}, u32[]{:S(2)}) collective-permute-start(bf16[8,2880]{1,0:T(8,128)(2,1)S(1)} %get-tuple-element.20), channel_id=1, source_target_pairs={{0,1},{1,0},{2,3},{3,2},{4,5},{5,4},{6,7},{7,6},{8,9},{9,8},{10,11... | collective-permute-start | bytes 138248 | tf_op jit(solution)/shard_map/ppermute | solution.py:253
  7.9 0.0 copy-done.2
  7.9 0.0 copy-done.3
  7.9 0.0 copy-done.4
  7.9 0.0 slice-start.2
  8.0 0.1 select_reduce_fusion.weights_ref
  8.0 0.0 copy-start.1
  8.0 0.0 copy-start
  8.1 0.0 slice-start.1
  8.1 0.0 slice-start.3
  8.1 0.1 shard_map.146.table_ref
  8.2 0.7 %copy-done.1 = f32[2880]{0:T(1024)S(1)} copy-done((f32[2880]{0:T(1024)S(1)}, f32[2880]{0:T(1024)}, u32[]{:S(2)}) %copy-start.1) | copy-done | bytes 11544
  8.9 1.0 %collective-permute-done.received_ref = bf16[8,2880]{1,0:T(8,128)(2,1)S(1)} collective-permute-done((bf16[8,2880]{1,0:T(8,128)(2,1)S(1)}, bf16[8,2880]{1,0:T(8,128)(2,1)S(1)}, u32[]{:S(2)}, u32[]{:S(2)}) %collective-permute-start) | collective-permute-done | bytes 46112 | tf_op jit(solution)/shard_map/ppermute | solution.py:253
  9.9 0.0 copy-done
  9.9 0.1 shard_map.147
  10.1 4.2 %collective-permute-start.3 = (bf16[8,2944]{1,0:T(8,128)(2,1)S(1)}, bf16[8,2944]{1,0:T(8,128)(2,1)S(1)}, u32[]{:S(2)}, u32[]{:S(2)}) collective-permute-start(bf16[8,2944]{1,0:T(8,128)(2,1)S(1)} %get-tuple-element.22.refs_0_), channel_id=1, source_target_pairs={{0,12},{2,14},{4,8},{6,10},{8,4},{10,6},{12,0},{14,2},{1,13},{3,15... | collective-permute-start | bytes 141320 | tf_op jit(solution)/shard_map/ppermute | solution.py:393
  14.3 0.0 collective-permute-start.2
  14.3 0.6 %collective-permute-start.1 = (bf16[8,2944]{1,0:T(8,128)(2,1)S(1)}, bf16[8,2944]{1,0:T(8,128)(2,1)S(1)}, u32[]{:S(2)}, u32[]{:S(2)}) collective-permute-start(bf16[8,2944]{1,0:T(8,128)(2,1)S(1)} %get-tuple-element.22.refs_0_), channel_id=1, source_target_pairs={{0,4},{2,6},{4,0},{6,2},{8,12},{10,14},{12,8},{14,10},{1,5},{3,7},... | collective-permute-start | bytes 141320 | tf_op jit(solution)/shard_map/ppermute | solution.py:393
  14.9 1.4 %collective-permute-done.3.refs_3_ = bf16[8,2944]{1,0:T(8,128)(2,1)S(1)} collective-permute-done((bf16[8,2944]{1,0:T(8,128)(2,1)S(1)}, bf16[8,2944]{1,0:T(8,128)(2,1)S(1)}, u32[]{:S(2)}, u32[]{:S(2)}) %collective-permute-start.3) | collective-permute-done | bytes 47136 | tf_op jit(solution)/shard_map/ppermute | solution.py:393
  16.3 2.9 %collective-permute-done.2.refs_2_ = bf16[8,2944]{1,0:T(8,128)(2,1)S(1)} collective-permute-done((bf16[8,2944]{1,0:T(8,128)(2,1)S(1)}, bf16[8,2944]{1,0:T(8,128)(2,1)S(1)}, u32[]{:S(2)}, u32[]{:S(2)}) %collective-permute-start.2) | collective-permute-done | bytes 47136 | tf_op jit(solution)/shard_map/ppermute | solution.py:393
  19.2 0.0 collective-permute-done.1.refs_1_
  19.3 0.1 collective-permute-start.4
  19.3 0.0 slice-done
  19.3 0.0 slice-done.1
  19.4 0.0 slice-start.4
  19.4 0.5 %shard_map.150.refs_4_ = bf16[1,2880,208]{2,1,0:T(8,128)(2,1)S(1)} custom-call(bf16[1,720,2880]{2,1,0:T(8,128)(2,1)S(1)} %bitcast.15), custom_call_target="tpu_custom_call" | custom-call | flops 1 | bytes 1 | tf_op jit(solution)/shard_map/pallas_call | solution.py:54
  19.8 0.0 slice-done.2
  19.8 0.0 slice-done.3
  19.9 0.0 slice-start.5
  19.9 2.0 %shard_map.149 = (bf16[1,2880,720]{2,1,0:T(8,128)(2,1)S(1)}, bf16[1,2880,512]{2,1,0:T(8,128)(2,1)S(1)}) custom-call(bf16[1,720,2880]{2,1,0:T(8,128)(2,1)S(1)} %bitcast.19, bf16[1,720,2880]{2,1,0:T(8,128)(2,1)S(1)} %bitcast.16), custom_call_target="tpu_custom_call" | custom-call | flops 1 | bytes 1 | tf_op jit(solution)/shard_map/pallas_call | solution.py:54
  21.9 0.0 collective-permute-done.4.refs_1_
  21.9 0.0 slice-done.4
  21.9 0.0 slice-done.5
  21.9 2.3 %shard_map.151 = (f32[32,2880]{1,0:T(8,128)S(1)}, bf16[32,2880]{1,0:T(8,128)(2,1)S(1)}) custom-call(bf16[32,2944]{1,0:T(8,128)(2,1)S(1)} %shard_map.148.refs_0_, bf16[32,2944]{1,0:T(8,128)(2,1)S(1)} %collective-permute-done.4.refs_1_, bf16[1,2880,720]{2,1,0:T(8,128)(2,1)S(1)} %get-tuple-element.23.refs_2_, ...), custom_call_target="tpu_custom_call" | custom-call | flops 796262400 | bytes 12441600 | tf_op jit(solution)/shard_map/pallas_call | solution.py:54
  24.3 0.5 %collective-permute-start.5 = (bf16[32,2880]{1,0:T(8,128)(2,1)S(1)}, bf16[32,2880]{1,0:T(8,128)(2,1)S(1)}, u32[]{:S(2)}, u32[]{:S(2)}) collective-permute-start(bf16[32,2880]{1,0:T(8,128)(2,1)S(1)} %get-tuple-element.26), channel_id=1, source_target_pairs={{0,2},{2,0},{4,6},{6,4},{8,10},{10,8},{12,14},{14,12},{1,3},{3,1},... | collective-permute-start | bytes 552968 | tf_op jit(solution)/shard_map/ppermute | solution.py:396
  24.8 1.1 %collective-permute-done.5.received_ref = bf16[32,2880]{1,0:T(8,128)(2,1)S(1)} collective-permute-done((bf16[32,2880]{1,0:T(8,128)(2,1)S(1)}, bf16[32,2880]{1,0:T(8,128)(2,1)S(1)}, u32[]{:S(2)}, u32[]{:S(2)}) %collective-permute-start.5) | collective-permute-done | bytes 184352 | tf_op jit(solution)/shard_map/ppermute | solution.py:396
  25.9 0.2 collective-permute-start.6
  26.1 2.0 %collective-permute-start.7 = (bf16[8,2880]{1,0:T(8,128)(2,1)S(1)}, bf16[8,2880]{1,0:T(8,128)(2,1)S(1)}, u32[]{:S(2)}, u32[]{:S(2)}) collective-permute-start(bf16[8,2880]{1,0:T(8,128)(2,1)S(1)} %get-tuple-element.29), channel_id=1, source_target_pairs={{0,8},{2,10},{4,12},{6,14},{8,0},{10,2},{12,4},{14,6},{1,9},{3,11}... | collective-permute-start | bytes 138248 | tf_op jit(solution)/shard_map/ppermute | solution.py:393
  28.1 2.3 %collective-permute-start.8 = (bf16[8,2880]{1,0:T(8,128)(2,1)S(1)}, bf16[8,2880]{1,0:T(8,128)(2,1)S(1)}, u32[]{:S(2)}, u32[]{:S(2)}) collective-permute-start(bf16[8,2880]{1,0:T(8,128)(2,1)S(1)} %get-tuple-element.30), channel_id=1, source_target_pairs={{0,12},{2,14},{4,8},{6,10},{8,4},{10,6},{12,0},{14,2},{1,13},{3,15... | collective-permute-start | bytes 138248 | tf_op jit(solution)/shard_map/ppermute | solution.py:393
  30.4 0.7 %collective-permute-done.6.refs_1_ = bf16[8,2880]{1,0:T(8,128)(2,1)S(1)} collective-permute-done((bf16[8,2880]{1,0:T(8,128)(2,1)S(1)}, bf16[8,2880]{1,0:T(8,128)(2,1)S(1)}, u32[]{:S(2)}, u32[]{:S(2)}) %collective-permute-start.6) | collective-permute-done | bytes 46112 | tf_op jit(solution)/shard_map/ppermute | solution.py:393
  31.0 0.0 collective-permute-done.7.refs_2_
  31.1 2.9 %collective-permute-done.8.refs_3_ = bf16[8,2880]{1,0:T(8,128)(2,1)S(1)} collective-permute-done((bf16[8,2880]{1,0:T(8,128)(2,1)S(1)}, bf16[8,2880]{1,0:T(8,128)(2,1)S(1)}, u32[]{:S(2)}, u32[]{:S(2)}) %collective-permute-start.8) | collective-permute-done | bytes 46112 | tf_op jit(solution)/shard_map/ppermute | solution.py:393
  34.0 0.2 shard_map.153
  34.1 1.6 %collective-permute-start.9 = (bf16[8,1440]{1,0:T(8,128)(2,1)S(1)}, bf16[8,1440]{1,0:T(8,128)(2,1)S(1)}, u32[]{:S(2)}, u32[]{:S(2)}) collective-permute-start(bf16[8,1440]{1,0:T(8,128)(2,1)S(1)} %get-tuple-element.32), channel_id=1, source_target_pairs={{0,1},{1,0},{2,3},{3,2},{4,5},{5,4},{6,7},{7,6},{8,9},{9,8},{10,11... | collective-permute-start | bytes 69128 | tf_op jit(solution)/shard_map/ppermute | solution.py:472
  35.7 2.3 %collective-permute-done.9 = bf16[8,1440]{1,0:T(8,128)(2,1)S(1)} collective-permute-done((bf16[8,1440]{1,0:T(8,128)(2,1)S(1)}, bf16[8,1440]{1,0:T(8,128)(2,1)S(1)}, u32[]{:S(2)}, u32[]{:S(2)}) %collective-permute-start.9) | collective-permute-done | bytes 23072 | tf_op jit(solution)/shard_map/ppermute | solution.py:472
  38.0 0.6 %add_convert_fusion = bf16[8,1440]{1,0:T(8,128)(2,1)} fusion(f32[8,1440]{1,0:T(8,128)S(1)} %get-tuple-element.31, bf16[8,1440]{1,0:T(8,128)(2,1)S(1)} %collective-permute-done.9), kind=kLoop, calls=%fused_computation | loop fusion | flops 34560 | bytes 92160 | tf_op jit(solution)/shard_map/convert_element_type | solution.py:473
  (9 shorter events, 0.1 us)
Async XLA Ops:
  0.0 7.9 %copy-start.2 = (f32[8,4]{0,1:T(4,128)S(1)}, f32[8,4]{0,1:T(4,128)}, u32[]{:S(2)}) copy-start(f32[8,4]{0,1:T(4,128)} %param.25) | copy-start | bytes 388
  0.0 7.9 %copy-start.3 = (s32[8,4]{0,1:T(4,128)S(1)}, s32[8,4]{0,1:T(4,128)}, u32[]{:S(2)}) copy-start(s32[8,4]{0,1:T(4,128)} %param.26) | copy-start | bytes 388
  0.0 7.9 %copy-start.4 = (s32[8,4]{0,1:T(4,128)S(1)}, s32[8,4]{0,1:T(4,128)}, u32[]{:S(2)}) copy-start(s32[8,4]{0,1:T(4,128)} %param.24) | copy-start | bytes 388
  0.0 19.3 %slice-start = ((s8[4239360]{0:T(1024)(128)(4,1)}), s8[45056]{0:T(1024)(128)(4,1)S(1)}, s32[]{:S(2)}) async-start(s8[4239360]{0:T(1024)(128)(4,1)} %bitcast.13), calls=%async_computation | async-start | bytes 90112
  4.8 5.1 %collective-permute-start = (bf16[8,2880]{1,0:T(8,128)(2,1)S(1)}, bf16[8,2880]{1,0:T(8,128)(2,1)S(1)}, u32[]{:S(2)}, u32[]{:S(2)}) collective-permute-start(bf16[8,2880]{1,0:T(8,128)(2,1)S(1)} %get-tuple-element.20), channel_id=1, source_target_pairs={{0,1},{1,0},{2,3},{3,2},{4,5},{5,4},{6,7},{7,6},{8,9},{9,8},{10,11... | collective-permute-start | bytes 138248 | tf_op jit(solution)/shard_map/ppermute | solution.py:253
  7.9 11.9 %slice-start.2 = ((s8[4239360]{0:T(1024)(128)(4,1)}), s8[4194304]{0:T(1024)(128)(4,1)S(1)}, s32[]{:S(2)}) async-start(s8[4239360]{0:T(1024)(128)(4,1)} %bitcast.17), calls=%async_computation.2 | async-start | bytes 8388608
  8.0 0.9 %copy-start.1 = (f32[2880]{0:T(1024)S(1)}, f32[2880]{0:T(1024)}, u32[]{:S(2)}) copy-start(f32[2880]{0:T(1024)} %param.23) | copy-start | bytes 34564
  8.0 1.9 %copy-start = (bf16[8,2880]{1,0:T(8,128)(2,1)S(1)}, bf16[8,2880]{1,0:T(8,128)(2,1)}, u32[]{:S(2)}) copy-start(bf16[8,2880]{1,0:T(8,128)(2,1)} %hidden_ref.1) | copy-start | bytes 138244
  8.1 11.3 %slice-start.1 = ((s8[4239360]{0:T(1024)(128)(4,1)}), s8[4194304]{0:T(1024)(128)(4,1)S(1)}, s32[]{:S(2)}) async-start(s8[4239360]{0:T(1024)(128)(4,1)} %bitcast.13), calls=%async_computation.1 | async-start | bytes 8388608
  8.1 11.8 %slice-start.3 = ((s8[4239360]{0:T(1024)(128)(4,1)}), s8[45056]{0:T(1024)(128)(4,1)S(1)}, s32[]{:S(2)}) async-start(s8[4239360]{0:T(1024)(128)(4,1)} %bitcast.17), calls=%async_computation.3 | async-start | bytes 90112
  10.1 6.2 %collective-permute-start.3 = (bf16[8,2944]{1,0:T(8,128)(2,1)S(1)}, bf16[8,2944]{1,0:T(8,128)(2,1)S(1)}, u32[]{:S(2)}, u32[]{:S(2)}) collective-permute-start(bf16[8,2944]{1,0:T(8,128)(2,1)S(1)} %get-tuple-element.22.refs_0_), channel_id=1, source_target_pairs={{0,12},{2,14},{4,8},{6,10},{8,4},{10,6},{12,0},{14,2},{1,13},{3,15... | collective-permute-start | bytes 141320 | tf_op jit(solution)/shard_map/ppermute | solution.py:393
  14.3 5.0 %collective-permute-start.2 = (bf16[8,2944]{1,0:T(8,128)(2,1)S(1)}, bf16[8,2944]{1,0:T(8,128)(2,1)S(1)}, u32[]{:S(2)}, u32[]{:S(2)}) collective-permute-start(bf16[8,2944]{1,0:T(8,128)(2,1)S(1)} %get-tuple-element.22.refs_0_), channel_id=1, source_target_pairs={{0,8},{2,10},{4,12},{6,14},{8,0},{10,2},{12,4},{14,6},{1,9},{3,11}... | collective-permute-start | bytes 141320 | tf_op jit(solution)/shard_map/ppermute | solution.py:393
  14.3 5.0 %collective-permute-start.1 = (bf16[8,2944]{1,0:T(8,128)(2,1)S(1)}, bf16[8,2944]{1,0:T(8,128)(2,1)S(1)}, u32[]{:S(2)}, u32[]{:S(2)}) collective-permute-start(bf16[8,2944]{1,0:T(8,128)(2,1)S(1)} %get-tuple-element.22.refs_0_), channel_id=1, source_target_pairs={{0,4},{2,6},{4,0},{6,2},{8,12},{10,14},{12,8},{14,10},{1,5},{3,7},... | collective-permute-start | bytes 141320 | tf_op jit(solution)/shard_map/ppermute | solution.py:393
  19.3 2.7 %collective-permute-start.4 = (bf16[32,2944]{1,0:T(8,128)(2,1)S(1)}, bf16[32,2944]{1,0:T(8,128)(2,1)S(1)}, u32[]{:S(2)}, u32[]{:S(2)}) collective-permute-start(bf16[32,2944]{1,0:T(8,128)(2,1)S(1)} %shard_map.148.refs_0_), channel_id=1, source_target_pairs={{0,2},{2,0},{4,6},{6,4},{8,10},{10,8},{12,14},{14,12},{1,3},{3,1},... | collective-permute-start | bytes 565256 | tf_op jit(solution)/shard_map/ppermute | solution.py:396
  19.4 2.6 %slice-start.4 = ((s8[4239360]{0:T(1024)(128)(4,1)}), s8[4194304]{0:T(1024)(128)(4,1)S(1)}, s32[]{:S(2)}) async-start(s8[4239360]{0:T(1024)(128)(4,1)} %bitcast.20), calls=%async_computation.4 | async-start | bytes 8388608
  19.9 2.1 %slice-start.5 = ((s8[4239360]{0:T(1024)(128)(4,1)}), s8[45056]{0:T(1024)(128)(4,1)S(1)}, s32[]{:S(2)}) async-start(s8[4239360]{0:T(1024)(128)(4,1)} %bitcast.20), calls=%async_computation.5 | async-start | bytes 90112
  24.3 1.6 %collective-permute-start.5 = (bf16[32,2880]{1,0:T(8,128)(2,1)S(1)}, bf16[32,2880]{1,0:T(8,128)(2,1)S(1)}, u32[]{:S(2)}, u32[]{:S(2)}) collective-permute-start(bf16[32,2880]{1,0:T(8,128)(2,1)S(1)} %get-tuple-element.26), channel_id=1, source_target_pairs={{0,2},{2,0},{4,6},{6,4},{8,10},{10,8},{12,14},{14,12},{1,3},{3,1},... | collective-permute-start | bytes 552968 | tf_op jit(solution)/shard_map/ppermute | solution.py:396
  25.9 5.1 %collective-permute-start.6 = (bf16[8,2880]{1,0:T(8,128)(2,1)S(1)}, bf16[8,2880]{1,0:T(8,128)(2,1)S(1)}, u32[]{:S(2)}, u32[]{:S(2)}) collective-permute-start(bf16[8,2880]{1,0:T(8,128)(2,1)S(1)} %get-tuple-element.28), channel_id=1, source_target_pairs={{0,4},{2,6},{4,0},{6,2},{8,12},{10,14},{12,8},{14,10},{1,5},{3,7},... | collective-permute-start | bytes 138248 | tf_op jit(solution)/shard_map/ppermute | solution.py:393
  26.1 5.0 %collective-permute-start.7 = (bf16[8,2880]{1,0:T(8,128)(2,1)S(1)}, bf16[8,2880]{1,0:T(8,128)(2,1)S(1)}, u32[]{:S(2)}, u32[]{:S(2)}) collective-permute-start(bf16[8,2880]{1,0:T(8,128)(2,1)S(1)} %get-tuple-element.29), channel_id=1, source_target_pairs={{0,8},{2,10},{4,12},{6,14},{8,0},{10,2},{12,4},{14,6},{1,9},{3,11}... | collective-permute-start | bytes 138248 | tf_op jit(solution)/shard_map/ppermute | solution.py:393
  28.1 5.9 %collective-permute-start.8 = (bf16[8,2880]{1,0:T(8,128)(2,1)S(1)}, bf16[8,2880]{1,0:T(8,128)(2,1)S(1)}, u32[]{:S(2)}, u32[]{:S(2)}) collective-permute-start(bf16[8,2880]{1,0:T(8,128)(2,1)S(1)} %get-tuple-element.30), channel_id=1, source_target_pairs={{0,12},{2,14},{4,8},{6,10},{8,4},{10,6},{12,0},{14,2},{1,13},{3,15... | collective-permute-start | bytes 138248 | tf_op jit(solution)/shard_map/ppermute | solution.py:393
  34.1 3.9 %collective-permute-start.9 = (bf16[8,1440]{1,0:T(8,128)(2,1)S(1)}, bf16[8,1440]{1,0:T(8,128)(2,1)S(1)}, u32[]{:S(2)}, u32[]{:S(2)}) collective-permute-start(bf16[8,1440]{1,0:T(8,128)(2,1)S(1)} %get-tuple-element.32), channel_id=1, source_target_pairs={{0,1},{1,0},{2,3},{3,2},{4,5},{5,4},{6,7},{7,6},{8,9},{9,8},{10,11... | collective-permute-start | bytes 69128 | tf_op jit(solution)/shard_map/ppermute | solution.py:472
